TPU v7x, 8 devices: a whole 2x2x1 slice. The times are simulated.
8 devices in a mesh: lev: 1 (over z), w: 8 (over y, x, core).
Axes of the slice: x: 2, y: 2, z: 1, core: 2. Of those that a mesh axis runs over, the one named last changes fastest.
Arguments:
- coef: float32 [512, 2, 32, 512], P('w', None, 'lev')
- legendre: float32 [512, 512, 768], replicated
- gauss_weight: float32 [768], replicated
Outputs:
- output 1: float32 [32, 768, 1024], P('lev', 'w')
- output 2: float32 [512, 2, 32, 512], P('w', None, 'lev')
All inputs are finite; a program needn't handle non-finite values.
Results may differ from a plain program's by a relative error of at most 0.001.
Values sent between devices are 32-bit elements.
A program may use at most 3.25 GiB of HBM per device.

v0:
```python
import jax
import jax.numpy as jnp
from jax import lax
from jax.sharding import PartitionSpec as P

FULL_PREC = lax.Precision.HIGHEST


def solution(mesh):
    group_size = mesh.shape['w']

    def per_device(coef, legendre, gauss_weight):
        wave_loc = coef.shape[0]
        wave_num = wave_loc * group_size
        lat_loc = legendre.shape[2] // group_size
        dev_idx = lax.axis_index('w')
        leg_own = lax.dynamic_slice_in_dim(legendre, dev_idx * wave_loc, wave_loc, axis=0)
        wt_own = lax.dynamic_slice_in_dim(gauss_weight, dev_idx * lat_loc, lat_loc, axis=0)
        fourier = jnp.einsum('mrkl,mlj->mrkj', coef, leg_own, preferred_element_type=jnp.float32, precision=FULL_PREC)
        fourier = lax.all_to_all(fourier, 'w', 3, 0, tiled=True)
        spec = jnp.transpose(lax.complex(fourier[:, 0], fourier[:, 1]), (1, 2, 0))
        grid = jnp.fft.irfft(spec, n=2 * wave_num, axis=-1)
        square_hat = jnp.fft.rfft(grid * grid, axis=-1)[:, :, :wave_num] * wt_own[None, :, None]
        re_im = jnp.stack([jnp.real(square_hat), jnp.imag(square_hat)], axis=0)
        re_im = jnp.transpose(re_im, (3, 0, 1, 2))
        re_im = lax.all_to_all(re_im, 'w', 0, 3, tiled=True)
        spec_out = jnp.einsum('mrkj,mlj->mrkl', re_im, leg_own, preferred_element_type=jnp.float32, precision=FULL_PREC)
        return grid, spec_out

    return jax.shard_map(per_device, mesh=mesh, in_specs=(P('w', None, 'lev', None), P(None, None, None), P(None)), out_specs=(P('lev', 'w', None), P('w', None, 'lev', None)), check_vma=False)
```

profile of v0, /device:TPU:1, one launch (start us, length us, event | category | flops | bytes accessed | tf_op | source)
XLA Modules:
  0.0 1089.7 jit_solution(460052509228503480)
XLA Ops:
  0.6 72.9 %fusion.16 = f32[64,2,32,768]{3,2,1,0:T(8,128)} fusion(f32[64,2,32,512]{3,2,1,0:T(8,128)} %param.3, f32[512,512,768]{2,1,0:T(8,128)} %param.4, s32[]{:T(128)S(6)} %select_n.6), kind=kOutput, calls=%fused_computation.37 | convolution fusion | flops 19327352832 | bytes 121634816 | tf_op jit(solution)/shard_map/mrkl,mlj->mrkj/dot_general | solution.py:19
  73.5 23.8 %copy.35 = f32[64,2,32,768]{0,2,1,3:T(8,128)} copy(f32[64,2,32,768]{3,2,1,0:T(8,128)} %fusion.16) | data formatting | bytes 25165824 | tf_op jit(solution)/shard_map/mrkl,mlj->mrkj/dot_general | solution.py:19
  97.3 20.5 %reshape.26 = f32[8,1,393216]{2,1,0:T(1,128)} reshape(f32[768,2,32,64]{3,2,1,0:T(8,128)} %bitcast.171) | data formatting | bytes 25165824
  124.2 13.1 %fusion.14 = f32[32,96,8,128]{3,2,1,0:T(8,128)} fusion(), kind=kOutput, calls=%fused_computation.35 | convolution fusion | flops 4831920128 | bytes 12582912 | tf_op jit(solution)/shard_map/jit(fft) | solution.py:23
  137.3 120.4 %all-to-all-done = f32[8,1,393216]{2,1,0:T(1,128)} async-done(((f32[8,1,393216]{2,1,0:T(1,128)}), f32[8,1,393216]{2,1,0:T(1,128)}, u32[]{:S(2)}, u32[]{:S(2)}) %all-to-all-start) | async-done | bytes 12582944 | tf_op jit(solution)/shard_map/all_to_all | solution.py:20
  258.1 37.1 %reduce = f32[8,393216]{1,0:T(8,128)} reduce(f32[8,1,393216]{2,1,0:T(1,128)} %all-to-all-done, f32[]{:T(128)} %broadcast.99), dimensions={1}, to_apply=%all_to_all.24.reduce_sub_computation | reduce | bytes 25165828 | tf_op jit(solution)/shard_map/all_to_all | solution.py:20
  295.2 22.6 %reshape.27 = f32[768,2,32,64]{3,2,1,0:T(8,128)} reshape(f32[8,393216]{1,0:T(8,128)} %reduce) | data formatting | bytes 25165824
  317.8 26.0 %copy.36 = f32[64,2,32,8,96]{4,2,1,0,3:T(8,128)} copy(f32[64,2,32,8,96]{0,2,1,4,3:T(8,128)} %bitcast.172) | data formatting | bytes 25165824 | tf_op jit(solution)/shard_map/all_to_all | solution.py:20
  384.6 20.1 %select_maximum_fusion = (f32[32,96,1024]{1,0,2:T(8,128)}, f32[32,96,1024]{1,0,2:T(8,128)}) fusion(f32[32,96,512]{1,0,2:T(8,128)} %get-tuple-element.9, f32[32,96,511]{1,0,2:T(8,128)} %reverse_negate_fusion, f32[32,96,511]{1,0,2:T(8,128)} %jit_fft_.448, f32[32,96,512]{1,0,2:T(8,128)S(1)} %bitcast.174), kind=kLoop, calls=%fused_computation.6 | loop fusion | flops 15728640 | bytes 50307072 | tf_op jit(solution)/shard_map/jit(fft) | solution.py:22
  404.7 21.7 %bitcast_add_fusion = f32[32,96,128,8]{1,3,2,0:T(8,128)} fusion(f32[32,96,1024]{1,0,2:T(8,128)} %get-tuple-element.12, f32[32,96,1024]{1,0,2:T(8,128)} %get-tuple-element.13), kind=kLoop, calls=%fused_computation.10 | loop fusion | flops 3145728 | bytes 37748736 | tf_op jit(solution)/shard_map/jit(fft) | solution.py:22
  426.3 16.3 %copy.39 = f32[32,96,128,8]{2,3,1,0:T(8,128)} copy(f32[32,96,128,8]{1,3,2,0:T(8,128)} %bitcast_add_fusion) | data formatting | bytes 25165824 | tf_op jit(solution)/shard_map/jit(fft) | solution.py:22
  442.6 15.4 %copy.41 = f32[32,96,128,8]{2,3,1,0:T(8,128)} copy(f32[32,96,128,8]{1,0,3,2:T(8,128)} %bitcast.168) | data formatting | bytes 25165824 | tf_op jit(solution)/shard_map/jit(fft) | solution.py:22
  458.0 15.2 %fusion.24 = f32[32,96,8,128]{3,2,1,0:T(8,128)} fusion(f32[32,96,128,8]{2,3,1,0:T(8,128)} %copy.41), kind=kOutput, calls=%fused_computation.43 | convolution fusion | flops 4831920128 | bytes 25165824 | tf_op jit(solution)/shard_map/jit(fft) | solution.py:22
  473.2 15.0 %copy.40 = f32[32,96,128,8]{2,3,1,0:T(8,128)} copy(f32[32,96,128,8]{1,0,3,2:T(8,128)} %bitcast.167) | data formatting | bytes 25165824 | tf_op jit(solution)/shard_map/jit(fft) | solution.py:22
  488.2 15.2 %fusion.26 = f32[32,96,8,128]{3,2,1,0:T(8,128)} fusion(f32[32,96,128,8]{2,3,1,0:T(8,128)} %copy.40), kind=kOutput, calls=%fused_computation.45 | convolution fusion | flops 4831920128 | bytes 25165824 | tf_op jit(solution)/shard_map/jit(fft) | solution.py:22
  503.4 27.7 %fusion.9 = (f32[32,96,128,8]{2,3,1,0:T(8,128)}, f32[32,96,128,8]{2,3,1,0:T(8,128)}) fusion(f32[128,8]{0,1:T(8,128)S(1)} %get-tuple-element.14, f32[128,8]{0,1:T(8,128)S(1)} %get-tuple-element.15, f32[32,96,8,128]{3,2,1,0:T(8,128)} %fusion.24, f32[32,96,8,128]{3,2,1,0:T(8,128)} %fusion.26, f32[32,96,128,8]{2,3,1,0:T(8,128)} %copy.39), kind=kOutput, calls=%fused_computation.20 | convolution fusion | flops 4857069568 | bytes 62922752 | tf_op jit(solution)/shard_map/jit(fft) | solution.py:22
  531.1 17.5 %fusion.64 = f32[32,96,128,8]{2,3,1,0:T(8,128)} fusion(f32[32,96,128,8]{2,3,1,0:T(8,128)} %get-tuple-element.5), kind=kOutput, calls=%fused_computation.76 | convolution fusion | flops 301990208 | bytes 25165824 | tf_op jit(solution)/shard_map/jit(fft) | solution.py:22
  548.6 16.7 %fusion.12 = f32[32,96,128,8]{2,3,1,0:T(8,128)} fusion(f32[32,96,128,8]{2,3,1,0:T(8,128)S(1)} %copy-done, f32[32,96,128,8]{2,3,1,0:T(8,128)} %get-tuple-element.4), kind=kOutput, calls=%fused_computation.28 | convolution fusion | flops 305135872 | bytes 37748736 | tf_op jit(solution)/shard_map/jit(fft) | solution.py:22
  565.2 27.2 %fusion.128 = (f32[32,96,8,128]{3,2,1,0:T(8,128)}, f32[32,96,8,128]{3,2,1,0:T(8,128)}) fusion(f32[32,96,128,8]{2,3,1,0:T(8,128)} %fusion.12, f32[32,96,128,8]{2,3,1,0:T(8,128)} %get-tuple-element.4, f32[32,96,128,8]{2,3,1,0:T(8,128)} %fusion.64), kind=kOutput, calls=%fused_computation.136 | convolution fusion | flops 320864576 | bytes 62914560 | tf_op jit(solution)/shard_map/jit(fft) | solution.py:22
  592.5 15.6 %copy.42 = f32[32,96,8,128]{1,3,2,0:T(8,128)} copy(f32[32,96,8,128]{3,2,1,0:T(8,128)} %get-tuple-element.10) | data formatting | bytes 25165824 | tf_op jit(solution)/shard_map/mul | solution.py:23
  608.1 16.2 %copy.43 = f32[32,96,128,8]{2,3,1,0:T(8,128)} copy(f32[32,96,128,8]{1,3,2,0:T(8,128)} %bitcast.175) | data formatting | bytes 25165824 | tf_op jit(solution)/shard_map/mul | solution.py:23
  624.3 15.6 %fusion.19 = f32[32,96,8,128]{3,2,1,0:T(8,128)} fusion(f32[32,96,128,8]{2,3,1,0:T(8,128)} %copy.43), kind=kOutput, calls=%fused_computation.38 | convolution fusion | flops 4831920128 | bytes 25165824 | tf_op jit(solution)/shard_map/jit(fft) | solution.py:23
  639.9 27.1 %fusion.7 = (f32[32,96,128,8]{2,3,1,0:T(8,128)}, f32[32,96,128,8]{2,3,1,0:T(8,128)}) fusion(f32[128,8]{0,1:T(8,128)S(1)} %copy-done.2, f32[128,8]{0,1:T(8,128)S(1)} %copy-done.3, f32[32,96,8,128]{3,2,1,0:T(8,128)} %fusion.19, f32[32,96,8,128]{3,2,1,0:T(8,128)} %fusion.14, f32[32,96,128,8]{2,3,1,0:T(8,128)} %copy.43), kind=kOutput, calls=%fused_computation.14 | convolution fusion | flops 4857069568 | bytes 62922752 | tf_op jit(solution)/shard_map/jit(fft) | solution.py:23
  667.1 18.7 %fusion.10 = f32[32,96,128,8]{2,3,1,0:T(8,128)} fusion(f32[32,96,128,8]{2,3,1,0:T(8,128)} %get-tuple-element.3, f32[32,96,128,8]{2,3,1,0:T(8,128)} %get-tuple-element.2), kind=kOutput, calls=%fused_computation.25 | convolution fusion | flops 305135872 | bytes 37748736 | tf_op jit(solution)/shard_map/jit(fft) | solution.py:23
  685.8 18.2 %subtract_bitcast_fusion = f32[32,96,8,128]{3,2,1,0:T(8,128)} fusion(f32[32,96,128,8]{2,3,1,0:T(8,128)} %fusion.10, f32[32,96,128,8]{2,3,1,0:T(8,128)} %get-tuple-element.2), kind=kOutput, calls=%fused_computation.24 | convolution fusion | flops 305135936 | bytes 37748736 | tf_op jit(solution)/shard_map/jit(fft) | solution.py:23
  704.0 15.2 %add_bitcast_fusion = f32[32,96,8,128]{3,2,1,0:T(8,128)} fusion(f32[32,96,128,8]{2,3,1,0:T(8,128)} %fusion.10, f32[32,96,128,8]{2,3,1,0:T(8,128)S(1)} %bitcast.170), kind=kOutput, calls=%fused_computation.23 | convolution fusion | flops 305135936 | bytes 37748736 | tf_op jit(solution)/shard_map/jit(fft) | solution.py:23
  731.2 12.2 %copy.65 = f32[32,96,8,128]{1,0,3,2:T(8,128)} copy(f32[32,96,8,128]{3,2,1,0:T(8,128)} %add_bitcast_fusion) | data formatting | bytes 25165824 | tf_op jit(solution)/shard_map/jit(fft) | solution.py:23
  765.3 13.6 %jit_fft_.515 = f32[32,96,1024]{2,1,0:T(8,128)} reshape(f32[32,96,8,128]{3,2,1,0:T(8,128)} %get-tuple-element.11) | data formatting | bytes 25165824 | tf_op jit(solution)/shard_map/jit(fft) | solution.py:22
  779.0 166.7 %all-to-all-done.1 = f32[512,2,32,96]{3,2,1,0:T(8,128)} async-done(((f32[512,2,32,96]{3,2,1,0:T(8,128)}), f32[512,2,32,96]{3,2,1,0:T(8,128)}, u32[]{:S(2)}, u32[]{:S(2)}) %all-to-all-start.1) | async-done | bytes 12582944 | tf_op jit(solution)/shard_map/all_to_all | solution.py:26
  945.7 21.1 %copy.48 = f32[64,2,32,8,96]{4,3,2,1,0:T(8,128)} copy(f32[64,2,32,8,96]{4,2,1,0,3:T(8,128)} %bitcast.56) | data formatting | bytes 25165824 | tf_op jit(solution)/shard_map/all_to_all | solution.py:26
  966.8 17.0 %all_to_all.31 = f32[64,2,32,768]{3,2,1,0:T(8,128)} reshape(f32[64,2,32,8,96]{4,3,2,1,0:T(8,128)} %copy.48) | data formatting | bytes 25165824 | tf_op jit(solution)/shard_map/all_to_all | solution.py:26
  983.9 105.4 %fusion = f32[64,2,32,512]{3,2,1,0:T(8,128)} fusion(f32[64,2,32,768]{3,2,1,0:T(8,128)} %all_to_all.31, f32[512,512,768]{2,1,0:T(8,128)} %param.4, s32[]{:T(128)S(6)} %select_n.6), kind=kOutput, calls=%fused_computation | convolution fusion | flops 19327352832 | bytes 121634816 | tf_op jit(solution)/shard_map/mrkj,mlj->mrkl/dot_general | solution.py:27
  (36 shorter events, 81.8 us)
Async XLA Ops:
  117.7 139.9 %all-to-all-start = ((f32[8,1,393216]{2,1,0:T(1,128)}), f32[8,1,393216]{2,1,0:T(1,128)}, u32[]{:S(2)}, u32[]{:S(2)}) async-start(f32[8,1,393216]{2,1,0:T(1,128)} %reshape.26), calls=%async_computation | async-start | bytes 25165824 | tf_op jit(solution)/shard_map/all_to_all | solution.py:20
  353.8 3.4 copy-start.1
  369.0 15.6 %slice-start.3 = ((s8[8388608]{0:T(1024)(128)(4,1)}), s8[4194304]{0:T(1024)(128)(4,1)S(1)}, s32[]{:S(2)}) async-start(s8[8388608]{0:T(1024)(128)(4,1)} %bitcast.173), calls=%async_computation.5 | async-start | bytes 8388608
  376.8 7.8 slice-start.4
  531.1 17.5 %copy-start = (f32[32,96,128,8]{2,3,1,0:T(8,128)S(1)}, f32[32,96,128,8]{2,3,1,0:T(8,128)}, u32[]{:S(2)}) copy-start(f32[32,96,128,8]{2,3,1,0:T(8,128)} %get-tuple-element.5) | copy-start | bytes 37748740
  624.3 15.7 %copy-start.2 = (f32[128,8]{0,1:T(8,128)S(1)}, f32[128,8]{0,1:T(8,128)}, u32[]{:S(2)}) copy-start(f32[128,8]{0,1:T(8,128)} %get-tuple-element.16) | copy-start | bytes 12292
  624.3 15.7 %copy-start.3 = (f32[128,8]{0,1:T(8,128)S(1)}, f32[128,8]{0,1:T(8,128)}, u32[]{:S(2)}) copy-start(f32[128,8]{0,1:T(8,128)} %get-tuple-element.17) | copy-start | bytes 12292
  667.1 36.9 %slice-start = ((s8[12582912]{0:T(1024)(128)(4,1)}), s8[4194304]{0:T(1024)(128)(4,1)S(1)}, s32[]{:S(2)}) async-start(s8[12582912]{0:T(1024)(128)(4,1)} %bitcast.169), calls=%async_computation.2 | async-start | bytes 8388608
  667.1 36.9 %slice-start.1 = ((s8[12582912]{0:T(1024)(128)(4,1)}), s8[4194304]{0:T(1024)(128)(4,1)S(1)}, s32[]{:S(2)}) async-start(s8[12582912]{0:T(1024)(128)(4,1)} %bitcast.169), calls=%async_computation.3 | async-start | bytes 8388608
  685.8 18.2 %slice-start.2 = ((s8[12582912]{0:T(1024)(128)(4,1)}), s8[4194304]{0:T(1024)(128)(4,1)S(1)}, s32[]{:S(2)}) async-start(s8[12582912]{0:T(1024)(128)(4,1)} %bitcast.169), calls=%async_computation.4 | async-start | bytes 8388608
  731.2 12.2 %copy-start.4 = (f32[96]{0:T(128)S(1)}, f32[96]{0:T(128)}, u32[]{:S(2)}) copy-start(f32[96]{0:T(128)} %dynamic_slice.7) | copy-start | bytes 1156
  756.7 189.0 %all-to-all-start.1 = ((f32[512,2,32,96]{3,2,1,0:T(8,128)}), f32[512,2,32,96]{3,2,1,0:T(8,128)}, u32[]{:S(2)}, u32[]{:S(2)}) async-start(f32[512,2,32,96]{3,2,1,0:T(8,128)} %maximum_bitcast_fusion), calls=%async_computation.1 | async-start | bytes 33554432 | tf_op jit(solution)/shard_map/all_to_all | solution.py:26
where the time goes:
time: 1100 us; the launch traced here: 1090 us
  matrix products  406 us (37%)
  waiting for transfers between devices  287 us (26%)
  local copies, waits for them, and re-layouts  282 us (26%)
  other arithmetic  101 us (9%)
  starting transfers between devices  13.2 us (1%)
    all_to_all x1, waiting for transfers between devices, per_device(): re_im = lax.all_to_all(re_im, 'w', 0, 3, tiled=True)  167 us
    all_to_all x1, waiting for transfers between devices, per_device(): fourier = lax.all_to_all(fourier, 'w', 3, 0, tiled=True)  120 us
    another operation x6, matrix products, per_device(): grid = jnp.fft.irfft(spec, n=2 * wave_num, axis=-1)  120 us
    another operation x6, matrix products, per_device(): jnp.fft.rfft(grid * grid, axis=-1)[:, :, :wave_num] * wt_own[None, :, None]  108 us
    dot_general x1, matrix products, per_device(): jnp.einsum('mrkj,mlj->mrkl', re_im, leg_own, preferred_element_type=jnp.f...  105 us
    another operation x7, local copies, waits for them, and re-layouts, per_device(): grid = jnp.fft.irfft(spec, n=2 * wave_num, axis=-1)  79.8 us
    dot_general x1, matrix products, per_device(): jnp.einsum('mrkl,mlj->mrkj', coef, leg_own, preferred_element_type=jnp.fl...  72.9 us
    another operation x4, other arithmetic, per_device(): grid = jnp.fft.irfft(spec, n=2 * wave_num, axis=-1)  49.6 us
  transfers between devices with their start and end apart: 2, of which 2 were waited for; matrix products, arithmetic and copies ran while one was open for 3% of the time, Pallas kernels for 0%

commit v1 on v0

v1 whole, which is shorter than its diff:
```python
import functools

import jax
import jax.numpy as jnp
import numpy as np
from jax import lax
from jax.experimental import pallas as pl
from jax.experimental.pallas import tpu as pltpu
from jax.sharding import PartitionSpec as P

DEVS = 8
WAVES = 512
OWN = WAVES // DEVS
LATS = 768
LAT = LATS // DEVS
LEVS = 32
LONS = 1024
HALF = LONS // 2
KK = 8
QQ = 4
LANES = QQ * LAT
CHUNK = 8
NB = 3
ROWS = 2 * KK
BF = jnp.bfloat16
F32 = jnp.float32


def split(x):
    hi = x.astype(BF)
    return hi, (x - hi.astype(F32)).astype(BF)


def dot3(a_hi, a_lo, b_hi, b_lo, dims):
    mm = functools.partial(lax.dot_general, dimension_numbers=(dims, ((), ())), preferred_element_type=F32)
    return mm(a_hi, b_hi) + (mm(a_hi, b_lo) + mm(a_lo, b_hi))


def barrier_all(me):
    sem = pltpu.get_barrier_semaphore()
    for o in range(1, DEVS):
        pl.semaphore_signal(sem, inc=1, device_id={'w': lax.rem(me + o, DEVS)}, device_id_type=pl.DeviceIdType.MESH)
    pl.semaphore_wait(sem, DEVS - 1)


def own_wave(t):
    return 2 * lax.rem(t, OWN // 2) + lax.div(t, OWN // 2)


def inverse_legendre(coef, leg, recv, cbuf, lbuf, stage, csem, lsem, ssem, rsem):
    me = lax.axis_index('w')
    barrier_all(me)

    def fetches(t):
        slot = lax.rem(t, NB)
        m = own_wave(t)
        return (pltpu.make_async_copy(coef.at[m], cbuf.at[slot], csem.at[slot]), pltpu.make_async_copy(leg.at[me * OWN + m], lbuf.at[slot], lsem.at[slot]))

    def sends(c):
        slot = lax.rem(c, 2)
        row = lax.div(c, 4) * (WAVES // 2) + me * (OWN // 2) + lax.rem(c, 4) * CHUNK
        row = pl.multiple_of(row, CHUNK)
        out = []
        for o in range(DEVS):
            dst = lax.rem(me + o, DEVS)
            src_ref, dst_ref = stage.at[slot, dst], recv.at[:, pl.ds(row, CHUNK), :]
            if o == 0:
                out.append(pltpu.make_async_copy(src_ref, dst_ref, ssem.at[slot, 0]))
            else:
                out.append(pltpu.make_async_remote_copy(src_ref=src_ref, dst_ref=dst_ref, send_sem=ssem.at[slot, o], recv_sem=rsem.at[lax.div(c, 4), o], device_id={'w': dst}, device_id_type=pl.DeviceIdType.MESH))
        return out

    def wait_sends(c):
        for o, copy in enumerate(sends(c)):
            if o == 0:
                copy.wait()
            else:
                copy.wait_send()

    for t in range(NB):
        for copy in fetches(t):
            copy.start()

    @pl.loop(0, OWN // CHUNK)
    def _(c):
        slot = lax.rem(c, 2)

        @pl.when(c >= 2)
        def _():
            wait_sends(c - 2)

        @pl.loop(0, CHUNK)
        def _(i):
            t = c * CHUNK + i
            for copy in fetches(t):
                copy.wait()
            buf = lax.rem(t, NB)
            c_hi, c_lo = split(cbuf[buf].reshape(2 * LEVS, WAVES))
            l_hi, l_lo = split(lbuf[buf])
            f = dot3(c_hi, c_lo, l_hi, l_lo, ((1,), (0,)))

            @pl.when(t + NB < OWN)
            def _():
                for copy in fetches(t + NB):
                    copy.start()

            for d in range(DEVS):
                cols = f[:, d * LAT:(d + 1) * LAT]
                for r in range(2):
                    row = r * LEVS
                    packed = jnp.concatenate([cols[row + q * KK:row + (q + 1) * KK] for q in range(QQ)], axis=1)
                    for h in range(KK):
                        stage[slot, d, r * KK + h, pl.ds(i, 1), :] = packed[h:h + 1]

        for copy in sends(c):
            copy.start()

    wait_sends(OWN // CHUNK - 2)
    wait_sends(OWN // CHUNK - 1)
    for o in range(1, DEVS):
        src = lax.rem(me - o + DEVS, DEVS)
        for par in range(2):
            part = recv.at[:, pl.ds(pl.multiple_of(par * (WAVES // 2) + src * (OWN // 2), OWN // 2), OWN // 2), :]
            pltpu.make_async_copy(part, part, rsem.at[par, o]).wait()


def longitudes(f_in, dft, dft_t, weight, grid_out, recv, fbuf, gbuf, stage, fsem, gsem, ssem, rsem):
    me = lax.axis_index('w')
    barrier_all(me)

    def fetches(kk):
        slot = lax.rem(kk, 2)
        return [pltpu.make_async_copy(f_in.at[r * KK + kk], fbuf.at[slot, r], fsem.at[slot, r]) for r in range(2)]

    def stores(kk):
        slot = lax.rem(kk, 2)
        return [pltpu.make_async_copy(gbuf.at[slot, pl.ds(q * LAT, LAT)], grid_out.at[q * KK + kk], gsem.at[slot, q]) for q in range(QQ)]

    def sends(kk):
        slot = lax.rem(kk, 2)
        out = []
        for o in range(DEVS):
            dst = lax.rem(me + o, DEVS)
            src_ref = stage.at[slot, :, :, pl.ds(pl.multiple_of(dst * (OWN // 2), OWN // 2), OWN // 2), :]
            dst_ref = recv.at[me, :, :, kk]
            if o == 0:
                out.append(pltpu.make_async_copy(src_ref, dst_ref, ssem.at[slot, 0]))
            else:
                out.append(pltpu.make_async_remote_copy(src_ref=src_ref, dst_ref=dst_ref, send_sem=ssem.at[slot, o], recv_sem=rsem.at[o], device_id={'w': dst}, device_id_type=pl.DeviceIdType.MESH))
        return out

    def wait_sends(kk):
        for o, copy in enumerate(sends(kk)):
            if o == 0:
                copy.wait()
            else:
                copy.wait_send()

    for copy in fetches(0):
        copy.start()

    @pl.loop(0, KK)
    def _(kk):
        slot = lax.rem(kk, 2)

        @pl.when(kk + 1 < KK)
        def _():
            for copy in fetches(kk + 1):
                copy.start()

        for copy in fetches(kk):
            copy.wait()

        @pl.when(kk >= 2)
        def _():
            wait_sends(kk - 2)
            for copy in stores(kk - 2):
                copy.wait()

        sums = []
        for par in range(2):
            rows = slice(par * (WAVES // 2), (par + 1) * (WAVES // 2))
            x = jnp.concatenate([fbuf[slot, 0, rows, :], fbuf[slot, 1, rows, :]], axis=0)
            x_hi, x_lo = split(x)
            sums.append(dot3(dft[par, 0], dft[par, 1], x_hi, x_lo, ((1,), (0,))))
        first, second = sums[0] + sums[1], sums[0] - sums[1]
        gbuf[slot, :, 0:HALF] = first.T
        gbuf[slot, :, HALF:LONS] = second.T
        for copy in stores(kk):
            copy.start()
        first, second = first * first, second * second
        for par, y in enumerate((first + second, first - second)):
            y_hi, y_lo = split(y)
            h = dot3(dft_t[par, 0], dft_t[par, 1], y_hi, y_lo, ((1,), (0,))) * weight[...]
            stage[slot, par, 0] = h[0:WAVES // 2]
            stage[slot, par, 1] = h[WAVES // 2:]
        for copy in sends(kk):
            copy.start()

    for kk in (KK - 2, KK - 1):
        wait_sends(kk)
        for copy in stores(kk):
            copy.wait()
    for o in range(1, DEVS):
        part = recv.at[lax.rem(me - o + DEVS, DEVS)]
        pltpu.make_async_copy(part, part, rsem.at[o]).wait()


def forward_legendre(h_in, leg, out, hbuf, lbuf, obuf, hsem, lsem, osem):
    me = lax.axis_index('w')

    def fetch_leg(t):
        slot = lax.rem(t, NB)
        return pltpu.make_async_copy(leg.at[me * OWN + own_wave(t)], lbuf.at[slot], lsem.at[slot])

    def fetch_h(c):
        slot = lax.rem(c, 2)
        row = pl.multiple_of(lax.rem(c, 4) * CHUNK, CHUNK)
        return pltpu.make_async_copy(h_in.at[:, lax.div(c, 4), :, :, pl.ds(row, CHUNK), :], hbuf.at[slot], hsem.at[slot])

    def store(t):
        slot = lax.rem(t, 2)
        return pltpu.make_async_copy(obuf.at[slot], out.at[own_wave(t)], osem.at[slot])

    fetch_h(0).start()
    for t in range(NB):
        fetch_leg(t).start()

    @pl.loop(0, OWN // CHUNK)
    def _(c):
        @pl.when(c + 1 < OWN // CHUNK)
        def _():
            fetch_h(c + 1).start()

        fetch_h(c).wait()
        hslot = lax.rem(c, 2)

        @pl.loop(0, CHUNK)
        def _(i):
            t = c * CHUNK + i
            rows = []
            for r in range(2):
                parts = []
                for d in range(DEVS):
                    parts.append(jnp.concatenate([hbuf[hslot, d, r, kk, pl.ds(i, 1), :] for kk in range(KK)], axis=0))
                for q in range(QQ):
                    rows.append(jnp.concatenate([p[:, q * LAT:(q + 1) * LAT] for p in parts], axis=1))
            h_hi, h_lo = split(jnp.concatenate(rows, axis=0))
            fetch_leg(t).wait()
            l_hi, l_lo = split(lbuf[lax.rem(t, NB)])

            @pl.when(t >= 2)
            def _():
                store(t - 2).wait()

            s = dot3(h_hi, h_lo, l_hi, l_lo, ((1,), (1,)))
            obuf[lax.rem(t, 2)] = s.reshape(2, LEVS, WAVES)
            store(t).start()

            @pl.when(t + NB < OWN)
            def _():
                fetch_leg(t + NB).start()

    store(OWN - 2).wait()
    store(OWN - 1).wait()


def dft_tables():
    n = np.arange(HALF)[:, None]
    tabs = []
    for par in range(2):
        m = np.arange(par, WAVES, 2)[None, :]
        ang = 2 * np.pi * ((m * n) % LONS) / LONS
        tabs.append(np.concatenate([np.cos(ang), -np.sin(ang)], axis=1))
    back = np.stack(tabs)
    scale = np.full((2, 1, WAVES), 2.0 / LONS)
    scale[0, 0, 0] = 1.0 / LONS
    scale[0, 0, WAVES // 2] = 0.0

    def halves(x):
        x = x.astype(np.float32)
        hi = x.astype(jnp.bfloat16)
        return np.stack([hi, (x - hi.astype(np.float32)).astype(jnp.bfloat16)], axis=1)

    return halves(back * scale), halves(np.swapaxes(back, 1, 2))


ANY = pl.BlockSpec(memory_space=pl.ANY)
VM = pl.BlockSpec(memory_space=pltpu.VMEM)
DMA = pltpu.SemaphoreType.DMA
LIMIT = 60 * 1024 * 1024


def solution(mesh):
    dft, dft_t = dft_tables()

    def per_device(coef, legendre, gauss_weight):
        me = lax.axis_index('w')
        own = lax.dynamic_slice_in_dim(gauss_weight, me * LAT, LAT, axis=0)
        weight = jnp.tile(own, QQ)[None, :]
        fourier = pl.pallas_call(
            inverse_legendre,
            out_shape=jax.ShapeDtypeStruct((ROWS, WAVES, LANES), F32),
            in_specs=[ANY, ANY],
            out_specs=ANY,
            scratch_shapes=[
                pltpu.VMEM((NB, 2, LEVS, WAVES), F32),
                pltpu.VMEM((NB, WAVES, LATS), F32),
                pltpu.VMEM((2, DEVS, ROWS, CHUNK, LANES), F32),
                DMA((NB,)), DMA((NB,)), DMA((2, DEVS)), DMA((2, DEVS)),
            ],
            compiler_params=pltpu.CompilerParams(collective_id=0, has_side_effects=True, vmem_limit_bytes=LIMIT),
            name='inverse_legendre',
        )(coef, legendre)
        grid, hats = pl.pallas_call(
            longitudes,
            out_shape=(jax.ShapeDtypeStruct((LEVS, LAT, LONS), F32), jax.ShapeDtypeStruct((DEVS, 2, 2, KK, OWN // 2, LANES), F32)),
            in_specs=[ANY, VM, VM, VM],
            out_specs=(ANY, ANY),
            scratch_shapes=[
                pltpu.VMEM((2, 2, WAVES, LANES), F32),
                pltpu.VMEM((2, LANES, LONS), F32),
                pltpu.VMEM((2, 2, 2, WAVES // 2, LANES), F32),
                DMA((2, 2)), DMA((2, QQ)), DMA((2, DEVS)), DMA((DEVS,)),
            ],
            compiler_params=pltpu.CompilerParams(collective_id=1, has_side_effects=True, vmem_limit_bytes=LIMIT),
            name='longitudes',
        )(fourier, dft, dft_t, weight)
        spec_out = pl.pallas_call(
            forward_legendre,
            out_shape=jax.ShapeDtypeStruct((OWN, 2, LEVS, WAVES), F32),
            in_specs=[ANY, ANY],
            out_specs=ANY,
            scratch_shapes=[
                pltpu.VMEM((2, DEVS, 2, KK, CHUNK, LANES), F32),
                pltpu.VMEM((NB, WAVES, LATS), F32),
                pltpu.VMEM((2, 2, LEVS, WAVES), F32),
                DMA((2,)), DMA((NB,)), DMA((2,)),
            ],
            compiler_params=pltpu.CompilerParams(vmem_limit_bytes=LIMIT),
            name='forward_legendre',
        )(hats, legendre)
        return grid, spec_out

    return jax.shard_map(per_device, mesh=mesh, in_specs=(P('w', None, 'lev', None), P(None, None, None), P(None)), out_specs=(P('lev', 'w', None), P('w', None, 'lev', None)), check_vma=False)
```

time: 1100 us -> 390 us (0.35)
  matrix products: 406 us -> 0 us
  Pallas kernels: 0 us -> 376 us
  waiting for transfers between devices: 287 us -> 0 us
  local copies, waits for them, and re-layouts: 282 us -> 13.5 us
  other arithmetic: 101 us -> 0 us
  starting transfers between devices: 13.2 us -> 0 us
    pallas_call x0 -> x3, Pallas kernels: none -> 376 us  [the longest x1 147 us: per_device(): pl.pallas_call(inverse_legendre, out_shape=jax.ShapeDtypeStruct((ROWS, WA...]
    all_to_all x2 -> x0, waiting for transfers between devices: 287 us -> none  [the longest x1 167 us: per_device(): re_im = lax.all_to_all(re_im, 'w', 0, 3, tiled=True)]
    another operation x12 -> x0, matrix products: 227 us -> none  [the longest x6 120 us: per_device(): grid = jnp.fft.irfft(spec, n=2 * wave_num, axis=-1)]
    dot_general x2 -> x0, matrix products: 178 us -> none  [the longest x1 105 us: per_device(): jnp.einsum('mrkj,mlj->mrkl', re_im, leg_own, preferred_element_type=jnp.f...]
    another operation x9 -> x2, local copies, waits for them, and re-layouts: 104 us -> 0.65 us  [per_device(): weight = jnp.tile(own, QQ)[None, :]]
    all_to_all x4 -> x0, local copies, waits for them, and re-layouts: 64.7 us -> none  [the longest x2 38.2 us: per_device(): re_im = lax.all_to_all(re_im, 'w', 0, 3, tiled=True)]
    another operation x6 -> x0, other arithmetic: 57.2 us -> none  [the longest x4 49.6 us: per_device(): grid = jnp.fft.irfft(spec, n=2 * wave_num, axis=-1)]
    all_to_all x1 -> x0, other arithmetic: 37.1 us -> none  [per_device(): fourier = lax.all_to_all(fourier, 'w', 3, 0, tiled=True)]
  transfers between devices with their start and end apart: 2 -> 0, of which waited for: 2 -> 0; matrix products, arithmetic and copies ran while one was open for 3% -> 0% of each run, Pallas kernels for 0% -> 0%
where the time goes in v1:
time: 390 us
  Pallas kernels  376 us (96%)
  local copies, waits for them, and re-layouts  13.5 us (3%)
    pallas_call x1, Pallas kernels, per_device(): pl.pallas_call(inverse_legendre, out_shape=jax.ShapeDtypeStruct((ROWS, WA...  147 us
    pallas_call x1, Pallas kernels, per_device(): pl.pallas_call(longitudes, out_shape=(jax.ShapeDtypeStruct((LEVS, LAT, LO...  146 us
    pallas_call x1, Pallas kernels, per_device(): pl.pallas_call(forward_legendre, out_shape=jax.ShapeDtypeStruct((OWN, 2,...  82.4 us
    unnamed x1, local copies, waits for them, and re-layouts  12.1 us

profile of v1, /device:TPU:1, one launch (start us, length us, event | category | flops | bytes accessed | tf_op | source)
XLA Modules:
  0.0 390.0 jit_solution(5013854341882309336)
XLA Ops:
  0.6 0.8 dynamic_slice.3
  1.4 0.6 broadcast_in_dim_tile.3.weight
  2.1 147.3 %inverse_legendre.1.f_in = f32[16,512,384]{2,1,0:T(8,128)} custom-call(f32[64,2,32,512]{3,2,1,0:T(8,128)} %coef.1, f32[512,512,768]{2,1,0:T(8,128)} %leg.3), custom_call_target="tpu_custom_call" | custom-call | tf_op jit(solution)/shard_map/inverse_legendre/pallas_call | solution.py:301
  149.4 146.1 %longitudes.1 = (f32[32,96,1024]{2,1,0:T(8,128)}, f32[8,2,2,8,32,384]{5,4,3,2,1,0:T(8,128)}) custom-call(f32[16,512,384]{2,1,0:T(8,128)} %inverse_legendre.1.f_in, bf16[2,2,512,512]{3,2,1,0:T(8,128)(2,1)} %constant.14.clone.dft, bf16[2,2,512,512]{3,2,1,0:T(8,128)(2,1)} %constant.15.clone.dft_t, f32[1,384]{1,0:T(1,128)} %broadcast_in_dim_tile.3.weight), custom_call_target="tpu_custom_call" | custom-call | tf_op jit(solution)/shard_map/longitudes/pallas_call | solution.py:315
  295.5 82.4 %forward_legendre.1 = f32[64,2,32,512]{3,2,1,0:T(8,128)} custom-call(f32[8,2,2,8,32,384]{5,4,3,2,1,0:T(8,128)} %get-tuple-element.5.h_in, f32[512,512,768]{2,1,0:T(8,128)} %leg.3), custom_call_target="tpu_custom_call" | custom-call | tf_op jit(solution)/shard_map/forward_legendre/pallas_call | solution.py:329
  377.9 12.1 %copy.8 = f32[32,96,1024]{2,1,0:T(8,128)} copy(f32[32,96,1024]{2,1,0:T(8,128)} %get-tuple-element.8) | data formatting | bytes 25165824
  (1 shorter events, 0.0 us)

commit v2 on v1

--- a/solution.py
+++ b/solution.py
@@ -21,6 +21,10 @@
 LANES = QQ * LAT
 CHUNK = 8
 NB = 3
+CHUNKS = OWN // CHUNK
+EARLY = 2
+AHEAD = 3
+EARLY_WAVES = OWN - CHUNK
 ROWS = 2 * KK
 BF = jnp.bfloat16
 F32 = jnp.float32
@@ -34,6 +38,14 @@
 def dot3(a_hi, a_lo, b_hi, b_lo, dims):
     mm = functools.partial(lax.dot_general, dimension_numbers=(dims, ((), ())), preferred_element_type=F32)
     return mm(a_hi, b_hi) + (mm(a_hi, b_lo) + mm(a_lo, b_hi))
+
+
+def dot_stacked(a, b, dims):
+    rows = a.shape[0]
+    (a_hi, a_lo), (b_hi, b_lo) = split(a), split(b)
+    mm = functools.partial(lax.dot_general, dimension_numbers=(dims, ((), ())), preferred_element_type=F32)
+    both = mm(jnp.concatenate([a_hi, a_lo], axis=0), b_hi)
+    return both[:rows] + (both[rows:] + mm(a_hi, b_lo))
 
 
 def barrier_all(me):
@@ -95,9 +107,7 @@
             for copy in fetches(t):
                 copy.wait()
             buf = lax.rem(t, NB)
-            c_hi, c_lo = split(cbuf[buf].reshape(2 * LEVS, WAVES))
-            l_hi, l_lo = split(lbuf[buf])
-            f = dot3(c_hi, c_lo, l_hi, l_lo, ((1,), (0,)))
+            f = dot_stacked(cbuf[buf].reshape(2 * LEVS, WAVES), lbuf[buf], ((1,), (0,)))
 
             @pl.when(t + NB < OWN)
             def _():
@@ -124,7 +134,16 @@
             pltpu.make_async_copy(part, part, rsem.at[par, o]).wait()
 
 
-def longitudes(f_in, dft, dft_t, weight, grid_out, recv, fbuf, gbuf, stage, fsem, gsem, ssem, rsem):
+def gather_rows(hbuf, i):
+    rows = []
+    for r in range(2):
+        parts = [jnp.concatenate([hbuf[d, r, kk, pl.ds(i, 1), :] for kk in range(KK)], axis=0) for d in range(DEVS)]
+        for q in range(QQ):
+            rows.append(jnp.concatenate([p[:, q * LAT:(q + 1) * LAT] for p in parts], axis=1))
+    return jnp.concatenate(rows, axis=0)
+
+
+def longitudes(f_in, leg, dft, dft_t, weight, grid_out, spec_out, last_out, fbuf, gbuf, hsend, hrecv, lbuf, obuf, fsem, gsem, ssem, asem, bsem, lsem, osem):
     me = lax.axis_index('w')
     barrier_all(me)
 
@@ -132,32 +151,49 @@
         slot = lax.rem(kk, 2)
         return [pltpu.make_async_copy(f_in.at[r * KK + kk], fbuf.at[slot, r], fsem.at[slot, r]) for r in range(2)]
 
+    def fetch_leg(t):
+        slot = lax.rem(t, NB)
+        return pltpu.make_async_copy(leg.at[me * OWN + own_wave(t)], lbuf.at[slot], lsem.at[slot])
+
     def stores(kk):
         slot = lax.rem(kk, 2)
         return [pltpu.make_async_copy(gbuf.at[slot, pl.ds(q * LAT, LAT)], grid_out.at[q * KK + kk], gsem.at[slot, q]) for q in range(QQ)]
 
-    def sends(kk):
-        slot = lax.rem(kk, 2)
-        out = []
+    def send(o, src_ref, dst_ref, sem):
+        if o == 0:
+            pltpu.make_async_copy(src_ref, dst_ref, sem).start()
+        else:
+            pltpu.make_async_remote_copy(src_ref=src_ref, dst_ref=dst_ref, send_sem=ssem.at[o], recv_sem=sem, device_id={'w': lax.rem(me + o, DEVS)}, device_id_type=pl.DeviceIdType.MESH).start()
+
+    def dst_rows(o, row, size):
+        return pl.ds(pl.multiple_of(lax.rem(me + o, DEVS) * (OWN // 2) + row, CHUNK), size)
+
+    def send_levels(kk):
         for o in range(DEVS):
-            dst = lax.rem(me + o, DEVS)
-            src_ref = stage.at[slot, :, :, pl.ds(pl.multiple_of(dst * (OWN // 2), OWN // 2), OWN // 2), :]
-            dst_ref = recv.at[me, :, :, kk]
-            if o == 0:
-                out.append(pltpu.make_async_copy(src_ref, dst_ref, ssem.at[slot, 0]))
-            else:
-                out.append(pltpu.make_async_remote_copy(src_ref=src_ref, dst_ref=dst_ref, send_sem=ssem.at[slot, o], recv_sem=rsem.at[o], device_id={'w': dst}, device_id_type=pl.DeviceIdType.MESH))
-        return out
-
-    def wait_sends(kk):
-        for o, copy in enumerate(sends(kk)):
-            if o == 0:
-                copy.wait()
-            else:
-                copy.wait_send()
+            send(o, hsend.at[:, :, kk, dst_rows(o, 0, OWN // 2), :], hrecv.at[me, :, :, kk], asem.at[o])
+
+    def chunk_at(ref, c):
+        row = pl.multiple_of(lax.rem(c, 4) * CHUNK, CHUNK)
+        return ref.at[lax.div(c, 4), :, pl.ds(EARLY, KK - EARLY), pl.ds(row, CHUNK), :]
+
+    def send_chunk(c):
+        row = lax.rem(c, 4) * CHUNK
+        for o in range(DEVS):
+            send(o, hsend.at[lax.div(c, 4), :, pl.ds(EARLY, KK - EARLY), dst_rows(o, row, CHUNK), :], chunk_at(hrecv.at[me], c), bsem.at[c, o])
+
+    def arrived(c):
+        for o in range(DEVS):
+            part = chunk_at(hrecv.at[lax.rem(me - o + DEVS, DEVS)], c)
+            pltpu.make_async_copy(part, part, bsem.at[c, o]).wait()
+
+    def store(t):
+        slot = lax.rem(t, 2)
+        return pltpu.make_async_copy(obuf.at[slot], spec_out.at[t], osem.at[slot])
 
     for copy in fetches(0):
         copy.start()
+    for t in range(NB):
+        fetch_leg(t).start()
 
     @pl.loop(0, KK)
     def _(kk):
@@ -173,7 +209,6 @@
 
         @pl.when(kk >= 2)
         def _():
-            wait_sends(kk - 2)
             for copy in stores(kk - 2):
                 copy.wait()
 
@@ -192,77 +227,108 @@
         for par, y in enumerate((first + second, first - second)):
             y_hi, y_lo = split(y)
             h = dot3(dft_t[par, 0], dft_t[par, 1], y_hi, y_lo, ((1,), (0,))) * weight[...]
-            stage[slot, par, 0] = h[0:WAVES // 2]
-            stage[slot, par, 1] = h[WAVES // 2:]
-        for copy in sends(kk):
-            copy.start()
-
+            hsend[par, 0, kk] = h[0:WAVES // 2]
+            hsend[par, 1, kk] = h[WAVES // 2:]
+
+        @pl.when(kk < EARLY)
+        def _():
+            send_levels(kk)
+
+    for c in range(AHEAD):
+        send_chunk(c)
     for kk in (KK - 2, KK - 1):
-        wait_sends(kk)
         for copy in stores(kk):
             copy.wait()
-    for o in range(1, DEVS):
-        part = recv.at[lax.rem(me - o + DEVS, DEVS)]
-        pltpu.make_async_copy(part, part, rsem.at[o]).wait()
-
-
-def forward_legendre(h_in, leg, out, hbuf, lbuf, obuf, hsem, lsem, osem):
-    me = lax.axis_index('w')
-
-    def fetch_leg(t):
-        slot = lax.rem(t, NB)
-        return pltpu.make_async_copy(leg.at[me * OWN + own_wave(t)], lbuf.at[slot], lsem.at[slot])
-
-    def fetch_h(c):
-        slot = lax.rem(c, 2)
-        row = pl.multiple_of(lax.rem(c, 4) * CHUNK, CHUNK)
-        return pltpu.make_async_copy(h_in.at[:, lax.div(c, 4), :, :, pl.ds(row, CHUNK), :], hbuf.at[slot], hsem.at[slot])
-
-    def store(t):
-        slot = lax.rem(t, 2)
-        return pltpu.make_async_copy(obuf.at[slot], out.at[own_wave(t)], osem.at[slot])
-
-    fetch_h(0).start()
-    for t in range(NB):
-        fetch_leg(t).start()
-
-    @pl.loop(0, OWN // CHUNK)
+    for o in range(DEVS):
+        part = hrecv.at[lax.rem(me - o + DEVS, DEVS), :, :, pl.ds(0, EARLY)]
+        pltpu.make_async_copy(part, part, asem.at[o]).wait()
+
+    @pl.loop(0, CHUNKS - 1)
     def _(c):
-        @pl.when(c + 1 < OWN // CHUNK)
+        arrived(c)
+
+        @pl.when(c + AHEAD < CHUNKS)
         def _():
-            fetch_h(c + 1).start()
-
-        fetch_h(c).wait()
-        hslot = lax.rem(c, 2)
+            send_chunk(c + AHEAD)
+
+        par, row = lax.div(c, 4), lax.rem(c, 4) * CHUNK
 
         @pl.loop(0, CHUNK)
         def _(i):
             t = c * CHUNK + i
-            rows = []
-            for r in range(2):
-                parts = []
-                for d in range(DEVS):
-                    parts.append(jnp.concatenate([hbuf[hslot, d, r, kk, pl.ds(i, 1), :] for kk in range(KK)], axis=0))
-                for q in range(QQ):
-                    rows.append(jnp.concatenate([p[:, q * LAT:(q + 1) * LAT] for p in parts], axis=1))
-            h_hi, h_lo = split(jnp.concatenate(rows, axis=0))
+            h = gather_rows(hrecv.at[:, par], row + i)
             fetch_leg(t).wait()
-            l_hi, l_lo = split(lbuf[lax.rem(t, NB)])
 
             @pl.when(t >= 2)
             def _():
                 store(t - 2).wait()
 
-            s = dot3(h_hi, h_lo, l_hi, l_lo, ((1,), (1,)))
-            obuf[lax.rem(t, 2)] = s.reshape(2, LEVS, WAVES)
+            obuf[lax.rem(t, 2)] = dot_stacked(h, lbuf[lax.rem(t, NB)], ((1,), (1,))).reshape(2, LEVS, WAVES)
             store(t).start()
 
-            @pl.when(t + NB < OWN)
+            @pl.when(t + NB < EARLY_WAVES)
             def _():
                 fetch_leg(t + NB).start()
 
-    store(OWN - 2).wait()
-    store(OWN - 1).wait()
+    arrived(CHUNKS - 1)
+    last = pltpu.make_async_copy(hrecv.at[:, 1, :, :, pl.ds(3 * CHUNK, CHUNK), :], last_out, asem.at[0])
+    last.start()
+    store(EARLY_WAVES - 2).wait()
+    store(EARLY_WAVES - 1).wait()
+    for o in range(1, DEVS):
+        part = hsend.at[:, :, :, dst_rows(o, 0, OWN // 2), :]
+        pltpu.make_async_copy(part, part, ssem.at[o]).wait()
+    last.wait()
+
+
+def finish(h_in, leg, grid_in, spec_in, grid_out, spec_out, hbuf, lbuf, obuf, gbuf, sbuf, hsem, lsem, osem, gsem, ssem, tsem):
+    me = lax.axis_index('w')
+    fetch_h = pltpu.make_async_copy(h_in, hbuf, hsem)
+    fetch_h.start()
+
+    def fetch_leg(i):
+        return pltpu.make_async_copy(leg.at[me * OWN + own_wave(EARLY_WAVES + i)], lbuf.at[i], lsem.at[i])
+
+    def grid_copy(i, back):
+        hbm = (grid_out if back else grid_in).at[pl.ds(i * QQ, QQ)]
+        return pltpu.make_async_copy(gbuf.at[i], hbm, gsem.at[1, i]) if back else pltpu.make_async_copy(hbm, gbuf.at[i], gsem.at[0, i])
+
+    def spec_fetch(i):
+        return pltpu.make_async_copy(spec_in.at[pl.ds(i * 7, 7)], sbuf.at[pl.ds(i * 7, 7)], ssem.at[i])
+
+    def spec_store(t):
+        return pltpu.make_async_copy(sbuf.at[t], spec_out.at[own_wave(t)], tsem.at[t])
+
+    def store(i):
+        return pltpu.make_async_copy(obuf.at[i], spec_out.at[own_wave(EARLY_WAVES + i)], osem.at[i])
+
+    fetch_leg(0).start()
+    fetch_leg(1).start()
+    for i in range(CHUNK):
+        grid_copy(i, False).start()
+        spec_fetch(i).start()
+        if i + 2 < CHUNK:
+            fetch_leg(i + 2).start()
+    fetch_h.wait()
+
+    @pl.loop(0, CHUNK)
+    def _(i):
+        h = gather_rows(hbuf, i)
+        fetch_leg(i).wait()
+        obuf[i] = dot_stacked(h, lbuf[i], ((1,), (1,))).reshape(2, LEVS, WAVES)
+        store(i).start()
+        grid_copy(i, False).wait()
+        grid_copy(i, True).start()
+        spec_fetch(i).wait()
+        for j in range(7):
+            spec_store(i * 7 + j).start()
+
+    @pl.loop(0, CHUNK)
+    def _(i):
+        store(i).wait()
+        grid_copy(i, True).wait()
+        for j in range(7):
+            spec_store(i * 7 + j).wait()
 
 
 def dft_tables():
@@ -312,34 +378,43 @@
             compiler_params=pltpu.CompilerParams(collective_id=0, has_side_effects=True, vmem_limit_bytes=LIMIT),
             name='inverse_legendre',
         )(coef, legendre)
-        grid, hats = pl.pallas_call(
+        grid_mid, spec_mid, last = pl.pallas_call(
             longitudes,
-            out_shape=(jax.ShapeDtypeStruct((LEVS, LAT, LONS), F32), jax.ShapeDtypeStruct((DEVS, 2, 2, KK, OWN // 2, LANES), F32)),
-            in_specs=[ANY, VM, VM, VM],
-            out_specs=(ANY, ANY),
+            out_shape=(
+                jax.ShapeDtypeStruct((LEVS, LAT, LONS), F32),
+                jax.ShapeDtypeStruct((EARLY_WAVES, 2, LEVS, WAVES), F32),
+                jax.ShapeDtypeStruct((DEVS, 2, KK, CHUNK, LANES), F32),
+            ),
+            in_specs=[ANY, ANY, VM, VM, VM],
+            out_specs=(ANY, ANY, ANY),
             scratch_shapes=[
                 pltpu.VMEM((2, 2, WAVES, LANES), F32),
                 pltpu.VMEM((2, LANES, LONS), F32),
-                pltpu.VMEM((2, 2, 2, WAVES // 2, LANES), F32),
-                DMA((2, 2)), DMA((2, QQ)), DMA((2, DEVS)), DMA((DEVS,)),
+                pltpu.VMEM((2, 2, KK, WAVES // 2, LANES), F32),
+                pltpu.VMEM((DEVS, 2, 2, KK, OWN // 2, LANES), F32),
+                pltpu.VMEM((NB, WAVES, LATS), F32),
+                pltpu.VMEM((2, 2, LEVS, WAVES), F32),
+                DMA((2, 2)), DMA((2, QQ)), DMA((DEVS,)), DMA((DEVS,)), DMA((CHUNKS, DEVS)), DMA((NB,)), DMA((2,)),
             ],
             compiler_params=pltpu.CompilerParams(collective_id=1, has_side_effects=True, vmem_limit_bytes=LIMIT),
             name='longitudes',
-        )(fourier, dft, dft_t, weight)
-        spec_out = pl.pallas_call(
-            forward_legendre,
-            out_shape=jax.ShapeDtypeStruct((OWN, 2, LEVS, WAVES), F32),
-            in_specs=[ANY, ANY],
-            out_specs=ANY,
+        )(fourier, legendre, dft, dft_t, weight)
+        grid, spec_out = pl.pallas_call(
+            finish,
+            out_shape=(jax.ShapeDtypeStruct((LEVS, LAT, LONS), F32), jax.ShapeDtypeStruct((OWN, 2, LEVS, WAVES), F32)),
+            in_specs=[ANY, ANY, ANY, ANY],
+            out_specs=(ANY, ANY),
             scratch_shapes=[
-                pltpu.VMEM((2, DEVS, 2, KK, CHUNK, LANES), F32),
-                pltpu.VMEM((NB, WAVES, LATS), F32),
-                pltpu.VMEM((2, 2, LEVS, WAVES), F32),
-                DMA((2,)), DMA((NB,)), DMA((2,)),
+                pltpu.VMEM((DEVS, 2, KK, CHUNK, LANES), F32),
+                pltpu.VMEM((CHUNK, WAVES, LATS), F32),
+                pltpu.VMEM((CHUNK, 2, LEVS, WAVES), F32),
+                pltpu.VMEM((CHUNK, QQ, LAT, LONS), F32),
+                pltpu.VMEM((EARLY_WAVES, 2, LEVS, WAVES), F32),
+                DMA, DMA((CHUNK,)), DMA((CHUNK,)), DMA((2, CHUNK)), DMA((CHUNK,)), DMA((EARLY_WAVES,)),
             ],
             compiler_params=pltpu.CompilerParams(vmem_limit_bytes=LIMIT),
-            name='forward_legendre',
-        )(hats, legendre)
+            name='finish',
+        )(last, legendre, grid_mid, spec_mid)
         return grid, spec_out
 
     return jax.shard_map(per_device, mesh=mesh, in_specs=(P('w', None, 'lev', None), P(None, None, None), P(None)), out_specs=(P('lev', 'w', None), P('w', None, 'lev', None)), check_vma=False)

time: 390 us -> 316 us (0.81)
  Pallas kernels: 376 us -> 314 us
  local copies, waits for them, and re-layouts: 13.5 us -> 1.42 us
    pallas_call x1, Pallas kernels: 82.4 us -> 18.5 us  [per_device(): pl.pallas_call(finish, out_shape=(jax.ShapeDtypeStruct((LEVS, LAT, LONS),...]
    unnamed x1 -> x0, local copies, waits for them, and re-layouts: 12.1 us -> none
where the time goes in v2:
time: 316 us
  Pallas kernels  314 us (99%)
    pallas_call x1, Pallas kernels, per_device(): pl.pallas_call(longitudes, out_shape=(jax.ShapeDtypeStruct((LEVS, LAT, LO...  149 us
    pallas_call x1, Pallas kernels, per_device(): pl.pallas_call(inverse_legendre, out_shape=jax.ShapeDtypeStruct((ROWS, WA...  147 us
    pallas_call x1, Pallas kernels, per_device(): pl.pallas_call(finish, out_shape=(jax.ShapeDtypeStruct((LEVS, LAT, LONS),...  18.5 us

profile of v2, /device:TPU:1, one launch (start us, length us, event | category | flops | bytes accessed | tf_op | source)
XLA Modules:
  0.0 316.2 jit_solution(15632064303258756389)
XLA Ops:
  0.6 0.8 dynamic_slice.3
  1.4 0.6 broadcast_in_dim_tile.3.weight
  2.1 146.8 %inverse_legendre.1.f_in = f32[16,512,384]{2,1,0:T(8,128)} custom-call(f32[64,2,32,512]{3,2,1,0:T(8,128)} %coef.1, f32[512,512,768]{2,1,0:T(8,128)} %leg.5), custom_call_target="tpu_custom_call" | custom-call | tf_op jit(solution)/shard_map/inverse_legendre/pallas_call | solution.py:367
  148.8 148.8 %longitudes.1 = (f32[32,96,1024]{2,1,0:T(8,128)}, f32[56,2,32,512]{3,2,1,0:T(8,128)}, f32[8,2,8,8,384]{4,3,2,1,0:T(8,128)}) custom-call(f32[16,512,384]{2,1,0:T(8,128)} %inverse_legendre.1.f_in, f32[512,512,768]{2,1,0:T(8,128)} %leg.5, bf16[2,2,512,512]{3,2,1,0:T(8,128)(2,1)} %constant.14.clone.dft, bf16[2,2,512,512]{3,2,1,0:T(8,128)(2,1)} %constant.15.clone.dft_t, ...), custom_call_target="tpu_custom_call" | custom-call | tf_op jit(solution)/shard_map/longitudes/pallas_call | solution.py:381
  297.7 18.5 %finish.1 = (f32[32,96,1024]{2,1,0:T(8,128)}, f32[64,2,32,512]{3,2,1,0:T(8,128)}) custom-call(f32[8,2,8,8,384]{4,3,2,1,0:T(8,128)} %get-tuple-element.5.h_in, f32[512,512,768]{2,1,0:T(8,128)} %leg.5, f32[32,96,1024]{2,1,0:T(8,128)} %get-tuple-element.6.grid_in, f32[56,2,32,512]{3,2,1,0:T(8,128)} %get-tuple-element.7.spec_in), custom_call_target="tpu_custom_call" | custom-call | tf_op jit(solution)/shard_map/finish/pallas_call | solution.py:402
  (1 shorter events, 0.0 us)

commit v3 on v2

v3 whole, which is shorter than its diff:
```python
import functools

import jax
import jax.numpy as jnp
import numpy as np
from jax import lax
from jax.experimental import pallas as pl
from jax.experimental.pallas import tpu as pltpu
from jax.sharding import PartitionSpec as P

DEVS = 8
WAVES = 512
OWN = WAVES // DEVS
LATS = 768
LAT = LATS // DEVS
LEVS = 32
LONS = 1024
HALF = LONS // 2
KK = 8
QQ = 4
LANES = QQ * LAT
CHUNK = 8
NB = 3
CHUNKS = OWN // CHUNK
FIRST = 4
EARLY = 2
AHEAD = 3
EARLY_WAVES = OWN - CHUNK
BF = jnp.bfloat16
F32 = jnp.float32


def split(x):
    hi = x.astype(BF)
    return hi, (x - hi.astype(F32)).astype(BF)


def dot3(a_hi, a_lo, b_hi, b_lo, dims):
    mm = functools.partial(lax.dot_general, dimension_numbers=(dims, ((), ())), preferred_element_type=F32)
    return mm(a_hi, b_hi) + (mm(a_hi, b_lo) + mm(a_lo, b_hi))


def dot_stacked(a, b, dims):
    rows = a.shape[0]
    (a_hi, a_lo), (b_hi, b_lo) = split(a), split(b)
    mm = functools.partial(lax.dot_general, dimension_numbers=(dims, ((), ())), preferred_element_type=F32)
    both = mm(jnp.concatenate([a_hi, a_lo], axis=0), b_hi)
    return both[:rows] + (both[rows:] + mm(a_hi, b_lo))


def barrier_all(me):
    sem = pltpu.get_barrier_semaphore()
    for o in range(1, DEVS):
        pl.semaphore_signal(sem, inc=1, device_id={'w': lax.rem(me + o, DEVS)}, device_id_type=pl.DeviceIdType.MESH)
    pl.semaphore_wait(sem, DEVS - 1)


def own_wave(t):
    return 2 * lax.rem(t, OWN // 2) + lax.div(t, OWN // 2)


def gather_rows(hbuf, i):
    rows = []
    for r in range(2):
        parts = [jnp.concatenate([hbuf[d, kk, r, pl.ds(i, 1), :] for kk in range(KK)], axis=0) for d in range(DEVS)]
        for q in range(QQ):
            rows.append(jnp.concatenate([p[:, q * LAT:(q + 1) * LAT] for p in parts], axis=1))
    return jnp.concatenate(rows, axis=0)


def transform(coef, leg, dft, dft_t, weight, frecv, grid_out, spec_out, last_out, cbuf, lbuf, fbuf, gbuf, both, hrecv, obuf, csem, lsem, fsem, gsem, osem, fs1, fr1, fs2, fr2, ssem, asem, bsem):
    me = lax.axis_index('w')
    barrier_all(me)

    def fetch_leg(t):
        slot = lax.rem(t, NB)
        return pltpu.make_async_copy(leg.at[me * OWN + own_wave(t)], lbuf.at[slot], lsem.at[slot])

    def fetch_coef(t):
        slot = lax.rem(t, NB)
        return pltpu.make_async_copy(coef.at[own_wave(t)], cbuf.at[slot], csem.at[slot])

    def target(o):
        return lax.rem(me + o, DEVS)

    def source(o):
        return lax.rem(me - o + DEVS, DEVS)

    def block(d, row=0, size=OWN):
        return pl.ds(pl.multiple_of(d * OWN + row, CHUNK), size)

    def move(o, src_ref, dst_ref, send_sem, recv_sem):
        if o == 0:
            pltpu.make_async_copy(src_ref, dst_ref, recv_sem).start()
        else:
            pltpu.make_async_remote_copy(src_ref=src_ref, dst_ref=dst_ref, send_sem=send_sem, recv_sem=recv_sem, device_id={'w': target(o)}, device_id_type=pl.DeviceIdType.MESH).start()

    def wait_for(part, sem):
        pltpu.make_async_copy(part, part, sem).wait()

    for t in range(NB):
        fetch_leg(t).start()
        fetch_coef(t).start()

    @pl.loop(0, CHUNKS)
    def _(c):
        @pl.loop(0, CHUNK)
        def _(i):
            t = c * CHUNK + i
            fetch_leg(t).wait()
            fetch_coef(t).wait()
            buf = lax.rem(t, NB)
            f = dot_stacked(cbuf[buf].reshape(2 * LEVS, WAVES), lbuf[buf], ((1,), (0,)))

            @pl.when(t + NB < OWN)
            def _():
                fetch_leg(t + NB).start()
                fetch_coef(t + NB).start()

            for d in range(DEVS):
                cols = f[:, d * LAT:(d + 1) * LAT]
                for r in range(2):
                    row = r * LEVS
                    packed = jnp.concatenate([cols[row + q * KK:row + (q + 1) * KK] for q in range(QQ)], axis=1)
                    for kk in range(KK):
                        both[kk, r, pl.ds(d * OWN + t, 1), :] = packed[kk:kk + 1]

        for o in range(DEVS):
            move(o, both.at[pl.ds(0, FIRST), :, block(target(o), c * CHUNK, CHUNK), :], frecv.at[pl.ds(0, FIRST), :, block(me, c * CHUNK, CHUNK), :], fs1.at[o], fr1.at[o])

    for kk in range(FIRST, KK):
        for o in range(DEVS):
            move(o, both.at[kk, :, block(target(o)), :], frecv.at[kk, :, block(me), :], fs2.at[kk, o], fr2.at[kk, o])
    for t in range(NB):
        fetch_leg(t).start()

    def stores(kk):
        slot = lax.rem(kk, 2)
        return [pltpu.make_async_copy(gbuf.at[slot, pl.ds(q * LAT, LAT)], grid_out.at[q * KK + kk], gsem.at[slot, q]) for q in range(QQ)]

    def dst_rows(o, row, size):
        return pl.ds(pl.multiple_of(target(o) * (OWN // 2) + row, CHUNK), size)

    def send_levels(kk):
        for o in range(DEVS):
            for par in range(2):
                move(o, both.at[kk, :, dst_rows(o, par * (WAVES // 2), OWN // 2), :], hrecv.at[me, par, kk], ssem.at[o], asem.at[o])

    def chunk_at(ref, c):
        row = pl.multiple_of(lax.rem(c, 4) * CHUNK, CHUNK)
        return ref.at[lax.div(c, 4), pl.ds(EARLY, KK - EARLY), :, pl.ds(row, CHUNK), :]

    def send_chunk(c):
        row = lax.div(c, 4) * (WAVES // 2) + lax.rem(c, 4) * CHUNK
        for o in range(DEVS):
            move(o, both.at[pl.ds(EARLY, KK - EARLY), :, dst_rows(o, row, CHUNK), :], chunk_at(hrecv.at[me], c), ssem.at[o], bsem.at[c, o])

    def arrived(c):
        for o in range(DEVS):
            wait_for(chunk_at(hrecv.at[source(o)], c), bsem.at[c, o])

    def store(t):
        slot = lax.rem(t, 2)
        return pltpu.make_async_copy(obuf.at[slot], spec_out.at[t], osem.at[slot])

    @pl.loop(0, KK)
    def _(kk):
        slot = lax.rem(kk, 2)

        @pl.when(kk == 0)
        def _():
            for o in range(DEVS):
                wait_for(frecv.at[pl.ds(0, FIRST), :, block(source(o)), :], fr1.at[o])
            for o in range(1, DEVS):
                wait_for(both.at[pl.ds(0, FIRST), :, block(target(o)), :], fs1.at[o])

        @pl.when(kk >= FIRST)
        def _():
            for o in range(DEVS):
                wait_for(frecv.at[kk, :, block(source(o)), :], fr2.at[kk, o])
            for o in range(1, DEVS):
                wait_for(both.at[kk, :, block(target(o)), :], fs2.at[kk, o])

        fetch = pltpu.make_async_copy(frecv.at[kk], fbuf, fsem)
        fetch.start()
        fetch.wait()

        @pl.when(kk >= 2)
        def _():
            for copy in stores(kk - 2):
                copy.wait()

        sums = []
        for par in range(2):
            x = jnp.concatenate([fbuf[r, d * OWN + par * (OWN // 2):d * OWN + (par + 1) * (OWN // 2), :] for r in range(2) for d in range(DEVS)], axis=0)
            x_hi, x_lo = split(x)
            sums.append(dot3(dft[par, 0], dft[par, 1], x_hi, x_lo, ((1,), (0,))))
        first, second = sums[0] + sums[1], sums[0] - sums[1]
        gbuf[slot, :, 0:HALF] = first.T
        gbuf[slot, :, HALF:LONS] = second.T
        for copy in stores(kk):
            copy.start()
        first, second = first * first, second * second
        for par, y in enumerate((first + second, first - second)):
            y_hi, y_lo = split(y)
            h = dot3(dft_t[par, 0], dft_t[par, 1], y_hi, y_lo, ((1,), (0,))) * weight[...]
            for r in range(2):
                both[kk, r, par * (WAVES // 2):(par + 1) * (WAVES // 2), :] = h[r * (WAVES // 2):(r + 1) * (WAVES // 2)]

        @pl.when(kk < EARLY)
        def _():
            send_levels(kk)

    for c in range(AHEAD):
        send_chunk(c)
    for kk in (KK - 2, KK - 1):
        for copy in stores(kk):
            copy.wait()
    for o in range(DEVS):
        wait_for(hrecv.at[source(o), :, pl.ds(0, EARLY)], asem.at[o])

    @pl.loop(0, CHUNKS - 1)
    def _(c):
        arrived(c)

        @pl.when(c + AHEAD < CHUNKS)
        def _():
            send_chunk(c + AHEAD)

        par, row = lax.div(c, 4), lax.rem(c, 4) * CHUNK

        @pl.loop(0, CHUNK)
        def _(i):
            t = c * CHUNK + i
            h = gather_rows(hrecv.at[:, par], row + i)
            fetch_leg(t).wait()

            @pl.when(t >= 2)
            def _():
                store(t - 2).wait()

            obuf[lax.rem(t, 2)] = dot_stacked(h, lbuf[lax.rem(t, NB)], ((1,), (1,))).reshape(2, LEVS, WAVES)
            store(t).start()

            @pl.when(t + NB < EARLY_WAVES)
            def _():
                fetch_leg(t + NB).start()

    arrived(CHUNKS - 1)
    last = pltpu.make_async_copy(hrecv.at[:, 1, :, :, pl.ds(3 * CHUNK, CHUNK), :], last_out, fsem)
    last.start()
    store(EARLY_WAVES - 2).wait()
    store(EARLY_WAVES - 1).wait()
    for o in range(1, DEVS):
        wait_for(both.at[:, :, block(target(o)), :], ssem.at[o])
    last.wait()


def finish(h_in, leg, grid_in, spec_in, grid_out, spec_out, hbuf, lbuf, obuf, gbuf, sbuf, hsem, lsem, osem, gsem, ssem, tsem):
    me = lax.axis_index('w')
    fetch_h = pltpu.make_async_copy(h_in, hbuf, hsem)
    fetch_h.start()

    def fetch_leg(i):
        return pltpu.make_async_copy(leg.at[me * OWN + own_wave(EARLY_WAVES + i)], lbuf.at[i], lsem.at[i])

    def grid_copy(i, back):
        hbm = (grid_out if back else grid_in).at[pl.ds(i * QQ, QQ)]
        return pltpu.make_async_copy(gbuf.at[i], hbm, gsem.at[1, i]) if back else pltpu.make_async_copy(hbm, gbuf.at[i], gsem.at[0, i])

    def spec_fetch(i):
        return pltpu.make_async_copy(spec_in.at[pl.ds(i * 7, 7)], sbuf.at[pl.ds(i * 7, 7)], ssem.at[i])

    def spec_store(t):
        return pltpu.make_async_copy(sbuf.at[t], spec_out.at[own_wave(t)], tsem.at[t])

    def store(i):
        return pltpu.make_async_copy(obuf.at[i], spec_out.at[own_wave(EARLY_WAVES + i)], osem.at[i])

    fetch_leg(0).start()
    fetch_leg(1).start()
    for i in range(CHUNK):
        grid_copy(i, False).start()
        spec_fetch(i).start()
        if i + 2 < CHUNK:
            fetch_leg(i + 2).start()
    fetch_h.wait()

    @pl.loop(0, CHUNK)
    def _(i):
        h = gather_rows(hbuf, i)
        fetch_leg(i).wait()
        obuf[i] = dot_stacked(h, lbuf[i], ((1,), (1,))).reshape(2, LEVS, WAVES)
        store(i).start()
        grid_copy(i, False).wait()
        grid_copy(i, True).start()
        spec_fetch(i).wait()
        for j in range(7):
            spec_store(i * 7 + j).start()

    @pl.loop(0, CHUNK)
    def _(i):
        store(i).wait()
        grid_copy(i, True).wait()
        for j in range(7):
            spec_store(i * 7 + j).wait()


def dft_tables():
    n = np.arange(HALF)[:, None]
    tabs = []
    for par in range(2):
        m = np.arange(par, WAVES, 2)[None, :]
        ang = 2 * np.pi * ((m * n) % LONS) / LONS
        tabs.append(np.concatenate([np.cos(ang), -np.sin(ang)], axis=1))
    back = np.stack(tabs)
    scale = np.full((2, 1, WAVES), 2.0 / LONS)
    scale[0, 0, 0] = 1.0 / LONS
    scale[0, 0, WAVES // 2] = 0.0

    def halves(x):
        x = x.astype(np.float32)
        hi = x.astype(jnp.bfloat16)
        return np.stack([hi, (x - hi.astype(np.float32)).astype(jnp.bfloat16)], axis=1)

    return halves(back * scale), halves(np.swapaxes(back, 1, 2))


ANY = pl.BlockSpec(memory_space=pl.ANY)
VM = pl.BlockSpec(memory_space=pltpu.VMEM)
DMA = pltpu.SemaphoreType.DMA
LIMIT = 60 * 1024 * 1024


def solution(mesh):
    dft, dft_t = dft_tables()

    def per_device(coef, legendre, gauss_weight):
        me = lax.axis_index('w')
        own = lax.dynamic_slice_in_dim(gauss_weight, me * LAT, LAT, axis=0)
        weight = jnp.tile(own, QQ)[None, :]
        _, grid_mid, spec_mid, last = pl.pallas_call(
            transform,
            out_shape=(
                jax.ShapeDtypeStruct((KK, 2, WAVES, LANES), F32),
                jax.ShapeDtypeStruct((LEVS, LAT, LONS), F32),
                jax.ShapeDtypeStruct((EARLY_WAVES, 2, LEVS, WAVES), F32),
                jax.ShapeDtypeStruct((DEVS, KK, 2, CHUNK, LANES), F32),
            ),
            in_specs=[ANY, ANY, VM, VM, VM],
            out_specs=(ANY, ANY, ANY, ANY),
            scratch_shapes=[
                pltpu.VMEM((NB, 2, LEVS, WAVES), F32),
                pltpu.VMEM((NB, WAVES, LATS), F32),
                pltpu.VMEM((2, WAVES, LANES), F32),
                pltpu.VMEM((2, LANES, LONS), F32),
                pltpu.VMEM((KK, 2, WAVES, LANES), F32),
                pltpu.VMEM((DEVS, 2, KK, 2, OWN // 2, LANES), F32),
                pltpu.VMEM((2, 2, LEVS, WAVES), F32),
                DMA((NB,)), DMA((NB,)), DMA, DMA((2, QQ)), DMA((2,)),
                DMA((DEVS,)), DMA((DEVS,)), DMA((KK, DEVS)), DMA((KK, DEVS)), DMA((DEVS,)), DMA((DEVS,)), DMA((CHUNKS, DEVS)),
            ],
            compiler_params=pltpu.CompilerParams(collective_id=0, has_side_effects=True, vmem_limit_bytes=LIMIT),
            name='transform',
        )(coef, legendre, dft, dft_t, weight)
        grid, spec_out = pl.pallas_call(
            finish,
            out_shape=(jax.ShapeDtypeStruct((LEVS, LAT, LONS), F32), jax.ShapeDtypeStruct((OWN, 2, LEVS, WAVES), F32)),
            in_specs=[ANY, ANY, ANY, ANY],
            out_specs=(ANY, ANY),
            scratch_shapes=[
                pltpu.VMEM((DEVS, KK, 2, CHUNK, LANES), F32),
                pltpu.VMEM((CHUNK, WAVES, LATS), F32),
                pltpu.VMEM((CHUNK, 2, LEVS, WAVES), F32),
                pltpu.VMEM((CHUNK, QQ, LAT, LONS), F32),
                pltpu.VMEM((EARLY_WAVES, 2, LEVS, WAVES), F32),
                DMA, DMA((CHUNK,)), DMA((CHUNK,)), DMA((2, CHUNK)), DMA((CHUNK,)), DMA((EARLY_WAVES,)),
            ],
            compiler_params=pltpu.CompilerParams(vmem_limit_bytes=LIMIT),
            name='finish',
        )(last, legendre, grid_mid, spec_mid)
        return grid, spec_out

    return jax.shard_map(per_device, mesh=mesh, in_specs=(P('w', None, 'lev', None), P(None, None, None), P(None)), out_specs=(P('lev', 'w', None), P('w', None, 'lev', None)), check_vma=False)
```

time: 316 us -> 308 us (0.975)
  Pallas kernels: 314 us -> 305 us
    pallas_call x2 -> x1, Pallas kernels: 296 us -> 287 us  [per_device(): pl.pallas_call(transform, out_shape=(jax.ShapeDtypeStruct((KK, 2, WAVES,...]
where the time goes in v3:
time: 308 us; the launch traced here: 307 us
  Pallas kernels  305 us (99%)
    pallas_call x1, Pallas kernels, per_device(): pl.pallas_call(transform, out_shape=(jax.ShapeDtypeStruct((KK, 2, WAVES,...  287 us
    pallas_call x1, Pallas kernels, per_device(): pl.pallas_call(finish, out_shape=(jax.ShapeDtypeStruct((LEVS, LAT, LONS),...  18.5 us

profile of v3, /device:TPU:1, one launch (start us, length us, event | category | flops | bytes accessed | tf_op | source)
XLA Modules:
  0.0 307.4 jit_solution(8917193377696002650)
XLA Ops:
  0.6 0.8 dynamic_slice.3
  1.4 0.6 broadcast_in_dim_tile.3.weight
  2.1 286.9 %transform.1 = (f32[8,2,512,384]{3,2,1,0:T(8,128)}, f32[32,96,1024]{2,1,0:T(8,128)}, f32[56,2,32,512]{3,2,1,0:T(8,128)}, f32[8,8,2,8,384]{4,3,2,1,0:T(8,128)}) custom-call(f32[64,2,32,512]{3,2,1,0:T(8,128)} %coef.1, f32[512,512,768]{2,1,0:T(8,128)} %leg.3, bf16[2,2,512,512]{3,2,1,0:T(8,128)(2,1)} %constant.14.clone.dft, ...), custom_call_target="tpu_custom_call" | custom-call | tf_op jit(solution)/shard_map/transform/pallas_call | solution.py:342
  288.9 18.5 %finish.1 = (f32[32,96,1024]{2,1,0:T(8,128)}, f32[64,2,32,512]{3,2,1,0:T(8,128)}) custom-call(f32[8,8,2,8,384]{4,3,2,1,0:T(8,128)} %get-tuple-element.5.h_in, f32[512,512,768]{2,1,0:T(8,128)} %leg.3, f32[32,96,1024]{2,1,0:T(8,128)} %get-tuple-element.6.grid_in, f32[56,2,32,512]{3,2,1,0:T(8,128)} %get-tuple-element.7.spec_in), custom_call_target="tpu_custom_call" | custom-call | tf_op jit(solution)/shard_map/finish/pallas_call | solution.py:366
  (1 shorter events, 0.0 us)

commit v4 on v3

--- a/solution.py
+++ b/solution.py
@@ -20,9 +20,9 @@
 QQ = 4
 LANES = QQ * LAT
 CHUNK = 8
-NB = 3
+NB = 5
 CHUNKS = OWN // CHUNK
-FIRST = 4
+FIRST = 6
 EARLY = 2
 AHEAD = 3
 EARLY_WAVES = OWN - CHUNK
@@ -68,7 +68,7 @@
     return jnp.concatenate(rows, axis=0)
 
 
-def transform(coef, leg, dft, dft_t, weight, frecv, grid_out, spec_out, last_out, cbuf, lbuf, fbuf, gbuf, both, hrecv, obuf, csem, lsem, fsem, gsem, osem, fs1, fr1, fs2, fr2, ssem, asem, bsem):
+def transform(coef, leg, dft, dft_t, weight, frecv, grid_out, spec_out, last_out, cbuf, lbuf, fbuf, both, hrecv, csem, lsem, fsem, fs1, fr1, fs2, fr2, ssem, asem, bsem):
     me = lax.axis_index('w')
     barrier_all(me)
 
@@ -134,10 +134,6 @@
     for t in range(NB):
         fetch_leg(t).start()
 
-    def stores(kk):
-        slot = lax.rem(kk, 2)
-        return [pltpu.make_async_copy(gbuf.at[slot, pl.ds(q * LAT, LAT)], grid_out.at[q * KK + kk], gsem.at[slot, q]) for q in range(QQ)]
-
     def dst_rows(o, row, size):
         return pl.ds(pl.multiple_of(target(o) * (OWN // 2) + row, CHUNK), size)
 
@@ -159,14 +155,8 @@
         for o in range(DEVS):
             wait_for(chunk_at(hrecv.at[source(o)], c), bsem.at[c, o])
 
-    def store(t):
-        slot = lax.rem(t, 2)
-        return pltpu.make_async_copy(obuf.at[slot], spec_out.at[t], osem.at[slot])
-
     @pl.loop(0, KK)
     def _(kk):
-        slot = lax.rem(kk, 2)
-
         @pl.when(kk == 0)
         def _():
             for o in range(DEVS):
@@ -185,21 +175,15 @@
         fetch.start()
         fetch.wait()
 
-        @pl.when(kk >= 2)
-        def _():
-            for copy in stores(kk - 2):
-                copy.wait()
-
         sums = []
         for par in range(2):
             x = jnp.concatenate([fbuf[r, d * OWN + par * (OWN // 2):d * OWN + (par + 1) * (OWN // 2), :] for r in range(2) for d in range(DEVS)], axis=0)
             x_hi, x_lo = split(x)
             sums.append(dot3(dft[par, 0], dft[par, 1], x_hi, x_lo, ((1,), (0,))))
         first, second = sums[0] + sums[1], sums[0] - sums[1]
-        gbuf[slot, :, 0:HALF] = first.T
-        gbuf[slot, :, HALF:LONS] = second.T
-        for copy in stores(kk):
-            copy.start()
+        for half, y in enumerate((first.T, second.T)):
+            for q in range(QQ):
+                grid_out[q * KK + kk, :, half * HALF:(half + 1) * HALF] = y[q * LAT:(q + 1) * LAT]
         first, second = first * first, second * second
         for par, y in enumerate((first + second, first - second)):
             y_hi, y_lo = split(y)
@@ -213,9 +197,6 @@
 
     for c in range(AHEAD):
         send_chunk(c)
-    for kk in (KK - 2, KK - 1):
-        for copy in stores(kk):
-            copy.wait()
     for o in range(DEVS):
         wait_for(hrecv.at[source(o), :, pl.ds(0, EARLY)], asem.at[o])
 
@@ -235,75 +216,57 @@
             h = gather_rows(hrecv.at[:, par], row + i)
             fetch_leg(t).wait()
 
-            @pl.when(t >= 2)
-            def _():
-                store(t - 2).wait()
-
-            obuf[lax.rem(t, 2)] = dot_stacked(h, lbuf[lax.rem(t, NB)], ((1,), (1,))).reshape(2, LEVS, WAVES)
-            store(t).start()
+            spec_out[t] = dot_stacked(h, lbuf[lax.rem(t, NB)], ((1,), (1,))).reshape(2, LEVS, WAVES)
 
             @pl.when(t + NB < EARLY_WAVES)
             def _():
                 fetch_leg(t + NB).start()
 
     arrived(CHUNKS - 1)
-    last = pltpu.make_async_copy(hrecv.at[:, 1, :, :, pl.ds(3 * CHUNK, CHUNK), :], last_out, fsem)
-    last.start()
-    store(EARLY_WAVES - 2).wait()
-    store(EARLY_WAVES - 1).wait()
+    last_out[...] = hrecv[:, 1, :, :, 3 * CHUNK:4 * CHUNK, :]
     for o in range(1, DEVS):
         wait_for(both.at[:, :, block(target(o)), :], ssem.at[o])
-    last.wait()
-
-
-def finish(h_in, leg, grid_in, spec_in, grid_out, spec_out, hbuf, lbuf, obuf, gbuf, sbuf, hsem, lsem, osem, gsem, ssem, tsem):
+
+
+def finish(h_in, leg, grid_in, spec_in, grid_out, spec_out, lbuf, obuf, lsem, osem, gsem, ssem):
     me = lax.axis_index('w')
-    fetch_h = pltpu.make_async_copy(h_in, hbuf, hsem)
-    fetch_h.start()
 
     def fetch_leg(i):
         return pltpu.make_async_copy(leg.at[me * OWN + own_wave(EARLY_WAVES + i)], lbuf.at[i], lsem.at[i])
 
-    def grid_copy(i, back):
-        hbm = (grid_out if back else grid_in).at[pl.ds(i * QQ, QQ)]
-        return pltpu.make_async_copy(gbuf.at[i], hbm, gsem.at[1, i]) if back else pltpu.make_async_copy(hbm, gbuf.at[i], gsem.at[0, i])
-
-    def spec_fetch(i):
-        return pltpu.make_async_copy(spec_in.at[pl.ds(i * 7, 7)], sbuf.at[pl.ds(i * 7, 7)], ssem.at[i])
-
-    def spec_store(t):
-        return pltpu.make_async_copy(sbuf.at[t], spec_out.at[own_wave(t)], tsem.at[t])
+    def grid_copy(i):
+        return pltpu.make_async_copy(grid_in.at[pl.ds(i * QQ, QQ)], grid_out.at[pl.ds(i * QQ, QQ)], gsem.at[i])
+
+    def spec_copy(t):
+        return pltpu.make_async_copy(spec_in.at[t], spec_out.at[own_wave(t)], ssem.at[t])
 
     def store(i):
         return pltpu.make_async_copy(obuf.at[i], spec_out.at[own_wave(EARLY_WAVES + i)], osem.at[i])
 
-    fetch_leg(0).start()
-    fetch_leg(1).start()
     for i in range(CHUNK):
-        grid_copy(i, False).start()
-        spec_fetch(i).start()
-        if i + 2 < CHUNK:
-            fetch_leg(i + 2).start()
-    fetch_h.wait()
+        fetch_leg(i).start()
+    for i in range(CHUNK):
+        grid_copy(i).start()
+
+    @pl.loop(0, EARLY_WAVES)
+    def _(t):
+        spec_copy(t).start()
 
     @pl.loop(0, CHUNK)
     def _(i):
-        h = gather_rows(hbuf, i)
+        h = gather_rows(h_in, i)
         fetch_leg(i).wait()
         obuf[i] = dot_stacked(h, lbuf[i], ((1,), (1,))).reshape(2, LEVS, WAVES)
         store(i).start()
-        grid_copy(i, False).wait()
-        grid_copy(i, True).start()
-        spec_fetch(i).wait()
-        for j in range(7):
-            spec_store(i * 7 + j).start()
 
     @pl.loop(0, CHUNK)
     def _(i):
         store(i).wait()
-        grid_copy(i, True).wait()
-        for j in range(7):
-            spec_store(i * 7 + j).wait()
+        grid_copy(i).wait()
+
+    @pl.loop(0, EARLY_WAVES)
+    def _(t):
+        spec_copy(t).wait()
 
 
 def dft_tables():
@@ -329,7 +292,8 @@
 ANY = pl.BlockSpec(memory_space=pl.ANY)
 VM = pl.BlockSpec(memory_space=pltpu.VMEM)
 DMA = pltpu.SemaphoreType.DMA
-LIMIT = 60 * 1024 * 1024
+LIMIT = 42 * 1024 * 1024
+LIMIT_END = 18 * 1024 * 1024
 
 
 def solution(mesh):
@@ -343,21 +307,19 @@
             transform,
             out_shape=(
                 jax.ShapeDtypeStruct((KK, 2, WAVES, LANES), F32),
-                jax.ShapeDtypeStruct((LEVS, LAT, LONS), F32),
-                jax.ShapeDtypeStruct((EARLY_WAVES, 2, LEVS, WAVES), F32),
-                jax.ShapeDtypeStruct((DEVS, KK, 2, CHUNK, LANES), F32),
+                pltpu.VMEM((LEVS, LAT, LONS), F32),
+                pltpu.VMEM((EARLY_WAVES, 2, LEVS, WAVES), F32),
+                pltpu.VMEM((DEVS, KK, 2, CHUNK, LANES), F32),
             ),
             in_specs=[ANY, ANY, VM, VM, VM],
-            out_specs=(ANY, ANY, ANY, ANY),
+            out_specs=(ANY, VM, VM, VM),
             scratch_shapes=[
                 pltpu.VMEM((NB, 2, LEVS, WAVES), F32),
                 pltpu.VMEM((NB, WAVES, LATS), F32),
                 pltpu.VMEM((2, WAVES, LANES), F32),
-                pltpu.VMEM((2, LANES, LONS), F32),
                 pltpu.VMEM((KK, 2, WAVES, LANES), F32),
                 pltpu.VMEM((DEVS, 2, KK, 2, OWN // 2, LANES), F32),
-                pltpu.VMEM((2, 2, LEVS, WAVES), F32),
-                DMA((NB,)), DMA((NB,)), DMA, DMA((2, QQ)), DMA((2,)),
+                DMA((NB,)), DMA((NB,)), DMA,
                 DMA((DEVS,)), DMA((DEVS,)), DMA((KK, DEVS)), DMA((KK, DEVS)), DMA((DEVS,)), DMA((DEVS,)), DMA((CHUNKS, DEVS)),
             ],
             compiler_params=pltpu.CompilerParams(collective_id=0, has_side_effects=True, vmem_limit_bytes=LIMIT),
@@ -366,17 +328,14 @@
         grid, spec_out = pl.pallas_call(
             finish,
             out_shape=(jax.ShapeDtypeStruct((LEVS, LAT, LONS), F32), jax.ShapeDtypeStruct((OWN, 2, LEVS, WAVES), F32)),
-            in_specs=[ANY, ANY, ANY, ANY],
+            in_specs=[VM, ANY, ANY, ANY],
             out_specs=(ANY, ANY),
             scratch_shapes=[
-                pltpu.VMEM((DEVS, KK, 2, CHUNK, LANES), F32),
                 pltpu.VMEM((CHUNK, WAVES, LATS), F32),
                 pltpu.VMEM((CHUNK, 2, LEVS, WAVES), F32),
-                pltpu.VMEM((CHUNK, QQ, LAT, LONS), F32),
-                pltpu.VMEM((EARLY_WAVES, 2, LEVS, WAVES), F32),
-                DMA, DMA((CHUNK,)), DMA((CHUNK,)), DMA((2, CHUNK)), DMA((CHUNK,)), DMA((EARLY_WAVES,)),
+                DMA((CHUNK,)), DMA((CHUNK,)), DMA((CHUNK,)), DMA((EARLY_WAVES,)),
             ],
-            compiler_params=pltpu.CompilerParams(vmem_limit_bytes=LIMIT),
+            compiler_params=pltpu.CompilerParams(vmem_limit_bytes=LIMIT_END),
             name='finish',
         )(last, legendre, grid_mid, spec_mid)
         return grid, spec_out

time: 308 us -> 302 us (0.981)
  Pallas kernels: 305 us -> 299 us
    pallas_call x1, Pallas kernels: 18.5 us -> 14.2 us  [per_device(): pl.pallas_call(finish, out_shape=(jax.ShapeDtypeStruct((LEVS, LAT, LONS),...]
where the time goes in v4:
time: 302 us; the launch traced here: 301 us
  Pallas kernels  299 us (99%)
    pallas_call x1, Pallas kernels, per_device(): pl.pallas_call(transform, out_shape=(jax.ShapeDtypeStruct((KK, 2, WAVES,...  285 us
    pallas_call x1, Pallas kernels, per_device(): pl.pallas_call(finish, out_shape=(jax.ShapeDtypeStruct((LEVS, LAT, LONS),...  14.2 us

profile of v4, /device:TPU:1, one launch (start us, length us, event | category | flops | bytes accessed | tf_op | source)
XLA Modules:
  0.0 301.4 jit_solution(16598752682699853843)
XLA Ops:
  0.6 0.8 dynamic_slice.3
  1.4 0.6 broadcast_in_dim_tile.3.weight
  2.1 285.1 %transform.1 = (f32[8,2,512,384]{3,2,1,0:T(8,128)}, f32[32,96,1024]{2,1,0:T(8,128)S(1)}, f32[56,2,32,512]{3,2,1,0:T(8,128)S(1)}, f32[8,8,2,8,384]{4,3,2,1,0:T(8,128)S(1)}) custom-call(f32[64,2,32,512]{3,2,1,0:T(8,128)} %coef.1, f32[512,512,768]{2,1,0:T(8,128)} %leg.3, bf16[2,2,512,512]{3,2,1,0:T(8,128)(2,1)} %constant.14.clone.dft, ...), custom_call_target="tpu_custom_call" | custom-call | tf_op jit(solution)/shard_map/transform/pallas_call | solution.py:306
  287.1 14.2 %finish.1 = (f32[32,96,1024]{2,1,0:T(8,128)}, f32[64,2,32,512]{3,2,1,0:T(8,128)}) custom-call(f32[8,8,2,8,384]{4,3,2,1,0:T(8,128)S(1)} %get-tuple-element.5.h_in, f32[512,512,768]{2,1,0:T(8,128)} %leg.3, f32[32,96,1024]{2,1,0:T(8,128)S(1)} %get-tuple-element.6.grid_in, f32[56,2,32,512]{3,2,1,0:T(8,128)S(1)} %get-tuple-element.7.spec_in), custom_call_target="tpu_custom_call" | custom-call | tf_op jit(solution)/shard_map/finish/pallas_call | solution.py:328
  (1 shorter events, 0.0 us)

commit v5 on v4

--- a/solution.py
+++ b/solution.py
@@ -48,11 +48,14 @@
     return both[:rows] + (both[rows:] + mm(a_hi, b_lo))
 
 
-def barrier_all(me):
+def barrier_signal(me):
     sem = pltpu.get_barrier_semaphore()
     for o in range(1, DEVS):
         pl.semaphore_signal(sem, inc=1, device_id={'w': lax.rem(me + o, DEVS)}, device_id_type=pl.DeviceIdType.MESH)
-    pl.semaphore_wait(sem, DEVS - 1)
+
+
+def barrier_wait():
+    pl.semaphore_wait(pltpu.get_barrier_semaphore(), DEVS - 1)
 
 
 def own_wave(t):
@@ -70,7 +73,7 @@
 
 def transform(coef, leg, dft, dft_t, weight, frecv, grid_out, spec_out, last_out, cbuf, lbuf, fbuf, both, hrecv, csem, lsem, fsem, fs1, fr1, fs2, fr2, ssem, asem, bsem):
     me = lax.axis_index('w')
-    barrier_all(me)
+    barrier_signal(me)
 
     def fetch_leg(t):
         slot = lax.rem(t, NB)
@@ -94,6 +97,11 @@
             pltpu.make_async_copy(src_ref, dst_ref, recv_sem).start()
         else:
             pltpu.make_async_remote_copy(src_ref=src_ref, dst_ref=dst_ref, send_sem=send_sem, recv_sem=recv_sem, device_id={'w': target(o)}, device_id_type=pl.DeviceIdType.MESH).start()
+
+    own_weight = weight[:, 0:LAT]
+    for d in range(1, DEVS):
+        own_weight = jnp.where(me == d, weight[:, d * LAT:(d + 1) * LAT], own_weight)
+    own_weight = jnp.concatenate([own_weight] * QQ, axis=1)
 
     def wait_for(part, sem):
         pltpu.make_async_copy(part, part, sem).wait()
@@ -124,6 +132,10 @@
                     packed = jnp.concatenate([cols[row + q * KK:row + (q + 1) * KK] for q in range(QQ)], axis=1)
                     for kk in range(KK):
                         both[kk, r, pl.ds(d * OWN + t, 1), :] = packed[kk:kk + 1]
+
+        @pl.when(c == 0)
+        def _():
+            barrier_wait()
 
         for o in range(DEVS):
             move(o, both.at[pl.ds(0, FIRST), :, block(target(o), c * CHUNK, CHUNK), :], frecv.at[pl.ds(0, FIRST), :, block(me, c * CHUNK, CHUNK), :], fs1.at[o], fr1.at[o])
@@ -187,7 +199,7 @@
         first, second = first * first, second * second
         for par, y in enumerate((first + second, first - second)):
             y_hi, y_lo = split(y)
-            h = dot3(dft_t[par, 0], dft_t[par, 1], y_hi, y_lo, ((1,), (0,))) * weight[...]
+            h = dot3(dft_t[par, 0], dft_t[par, 1], y_hi, y_lo, ((1,), (0,))) * own_weight
             for r in range(2):
                 both[kk, r, par * (WAVES // 2):(par + 1) * (WAVES // 2), :] = h[r * (WAVES // 2):(r + 1) * (WAVES // 2)]
 
@@ -300,9 +312,6 @@
     dft, dft_t = dft_tables()
 
     def per_device(coef, legendre, gauss_weight):
-        me = lax.axis_index('w')
-        own = lax.dynamic_slice_in_dim(gauss_weight, me * LAT, LAT, axis=0)
-        weight = jnp.tile(own, QQ)[None, :]
         _, grid_mid, spec_mid, last = pl.pallas_call(
             transform,
             out_shape=(
@@ -324,7 +333,7 @@
             ],
             compiler_params=pltpu.CompilerParams(collective_id=0, has_side_effects=True, vmem_limit_bytes=LIMIT),
             name='transform',
-        )(coef, legendre, dft, dft_t, weight)
+        )(coef, legendre, dft, dft_t, gauss_weight[None, :])
         grid, spec_out = pl.pallas_call(
             finish,
             out_shape=(jax.ShapeDtypeStruct((LEVS, LAT, LONS), F32), jax.ShapeDtypeStruct((OWN, 2, LEVS, WAVES), F32)),

time: 302 us -> 301 us (level)
  no operation moved by 1% of the time
where the time goes in v5:
time: 301 us; the launch traced here: 300 us
  Pallas kernels  298 us (99%)
    pallas_call x1, Pallas kernels, per_device(): pl.pallas_call(transform, out_shape=(jax.ShapeDtypeStruct((KK, 2, WAVES,...  284 us
    pallas_call x1, Pallas kernels, per_device(): pl.pallas_call(finish, out_shape=(jax.ShapeDtypeStruct((LEVS, LAT, LONS),...  14.2 us

profile of v5, /device:TPU:1, one launch (start us, length us, event | category | flops | bytes accessed | tf_op | source)
XLA Modules:
  0.0 300.3 jit_solution(16412419140007217295)
XLA Ops:
  0.6 1.3 broadcast_in_dim.3.weight
  1.9 284.2 %transform.1 = (f32[8,2,512,384]{3,2,1,0:T(8,128)}, f32[32,96,1024]{2,1,0:T(8,128)S(1)}, f32[56,2,32,512]{3,2,1,0:T(8,128)S(1)}, f32[8,8,2,8,384]{4,3,2,1,0:T(8,128)S(1)}) custom-call(f32[64,2,32,512]{3,2,1,0:T(8,128)} %coef.1, f32[512,512,768]{2,1,0:T(8,128)} %leg.3, bf16[2,2,512,512]{3,2,1,0:T(8,128)(2,1)} %constant.4.clone.dft, ...), custom_call_target="tpu_custom_call" | custom-call | tf_op jit(solution)/shard_map/transform/pallas_call | solution.py:315
  286.1 14.2 %finish.1 = (f32[32,96,1024]{2,1,0:T(8,128)}, f32[64,2,32,512]{3,2,1,0:T(8,128)}) custom-call(f32[8,8,2,8,384]{4,3,2,1,0:T(8,128)S(1)} %get-tuple-element.5.h_in, f32[512,512,768]{2,1,0:T(8,128)} %leg.3, f32[32,96,1024]{2,1,0:T(8,128)S(1)} %get-tuple-element.6.grid_in, f32[56,2,32,512]{3,2,1,0:T(8,128)S(1)} %get-tuple-element.7.spec_in), custom_call_target="tpu_custom_call" | custom-call | tf_op jit(solution)/shard_map/finish/pallas_call | solution.py:337

commit v6 on v5

--- a/solution.py
+++ b/solution.py
@@ -18,6 +18,7 @@
 HALF = LONS // 2
 KK = 8
 QQ = 4
+SIDE = 4
 LANES = QQ * LAT
 CHUNK = 8
 NB = 5
@@ -71,23 +72,41 @@
     return jnp.concatenate(rows, axis=0)
 
 
-def transform(coef, leg, dft, dft_t, weight, frecv, grid_out, spec_out, last_out, cbuf, lbuf, fbuf, both, hrecv, csem, lsem, fsem, fs1, fr1, fs2, fr2, ssem, asem, bsem):
+def whole(lbuf, slot):
+    return jnp.concatenate([lbuf[slot, 0], lbuf[slot, 1]], axis=1)
+
+
+def transform(coef, leg, dft, dft_t, weight, frecv, spec_out, last_out, lbuf, grid_out, cbuf, fbuf, both, hrecv, csem, hsem, lsem, fsem, fs1, fr1, fs2, fr2, ssem, asem, bsem):
     me = lax.axis_index('w')
     barrier_signal(me)
 
-    def fetch_leg(t):
+    row, col = lax.div(me, SIDE), lax.rem(me, SIDE)
+
+    def fetch_half(u):
+        t = lax.div(u, 2 * CHUNK) * CHUNK + lax.rem(u, CHUNK)
+        side = lax.rem(row + 1 + lax.rem(lax.div(u, CHUNK), 2), 2)
+        cols = pl.ds(pl.multiple_of(side * LANES, LANES), LANES)
+        buf = lax.rem(u, 2 * NB)
+        return pltpu.make_async_copy(leg.at[me * OWN + own_wave(t), :, cols], lbuf.at[lax.div(buf, 2), lax.rem(buf, 2)], hsem.at[buf])
+
+    def fetch_coef(u):
+        t = lax.div(u, 2 * CHUNK) * CHUNK + lax.rem(u, CHUNK)
+        slot = lax.rem(u, NB)
+        return pltpu.make_async_copy(coef.at[own_wave(t)], cbuf.at[slot], csem.at[slot])
+
+    def fetch_leg(t, half):
         slot = lax.rem(t, NB)
-        return pltpu.make_async_copy(leg.at[me * OWN + own_wave(t)], lbuf.at[slot], lsem.at[slot])
-
-    def fetch_coef(t):
-        slot = lax.rem(t, NB)
-        return pltpu.make_async_copy(coef.at[own_wave(t)], cbuf.at[slot], csem.at[slot])
+        cols = pl.ds(half * LANES, LANES)
+        return pltpu.make_async_copy(leg.at[me * OWN + own_wave(t), :, cols], lbuf.at[slot, half], lsem.at[slot, half])
+
+    def row_of(o):
+        return row if o < SIDE else 1 - row
 
     def target(o):
-        return lax.rem(me + o, DEVS)
+        return row_of(o) * SIDE + lax.rem(col + o, SIDE)
 
     def source(o):
-        return lax.rem(me - o + DEVS, DEVS)
+        return row_of(o) * SIDE + lax.rem(col - o + DEVS, SIDE)
 
     def block(d, row=0, size=OWN):
         return pl.ds(pl.multiple_of(d * OWN + row, CHUNK), size)
@@ -98,53 +117,64 @@
         else:
             pltpu.make_async_remote_copy(src_ref=src_ref, dst_ref=dst_ref, send_sem=send_sem, recv_sem=recv_sem, device_id={'w': target(o)}, device_id_type=pl.DeviceIdType.MESH).start()
 
-    own_weight = weight[:, 0:LAT]
+    weights = weight[...].reshape(1, LATS)
+    own_weight = weights[:, 0:LAT]
     for d in range(1, DEVS):
-        own_weight = jnp.where(me == d, weight[:, d * LAT:(d + 1) * LAT], own_weight)
+        own_weight = jnp.where(me == d, weights[:, d * LAT:(d + 1) * LAT], own_weight)
     own_weight = jnp.concatenate([own_weight] * QQ, axis=1)
 
     def wait_for(part, sem):
         pltpu.make_async_copy(part, part, sem).wait()
 
-    for t in range(NB):
-        fetch_leg(t).start()
-        fetch_coef(t).start()
+    for u in range(2 * NB):
+        fetch_half(u).start()
+    for u in range(NB):
+        fetch_coef(u).start()
 
     @pl.loop(0, CHUNKS)
     def _(c):
-        @pl.loop(0, CHUNK)
-        def _(i):
-            t = c * CHUNK + i
-            fetch_leg(t).wait()
-            fetch_coef(t).wait()
-            buf = lax.rem(t, NB)
-            f = dot_stacked(cbuf[buf].reshape(2 * LEVS, WAVES), lbuf[buf], ((1,), (0,)))
-
-            @pl.when(t + NB < OWN)
-            def _():
-                fetch_leg(t + NB).start()
-                fetch_coef(t + NB).start()
-
-            for d in range(DEVS):
-                cols = f[:, d * LAT:(d + 1) * LAT]
-                for r in range(2):
-                    row = r * LEVS
-                    packed = jnp.concatenate([cols[row + q * KK:row + (q + 1) * KK] for q in range(QQ)], axis=1)
-                    for kk in range(KK):
-                        both[kk, r, pl.ds(d * OWN + t, 1), :] = packed[kk:kk + 1]
-
-        @pl.when(c == 0)
-        def _():
-            barrier_wait()
-
-        for o in range(DEVS):
-            move(o, both.at[pl.ds(0, FIRST), :, block(target(o), c * CHUNK, CHUNK), :], frecv.at[pl.ds(0, FIRST), :, block(me, c * CHUNK, CHUNK), :], fs1.at[o], fr1.at[o])
+        for part in range(2):
+            side = lax.rem(row + 1 + part, 2)
+
+            @pl.loop(0, CHUNK)
+            def _(i):
+                u = (2 * c + part) * CHUNK + i
+                t = c * CHUNK + i
+                fetch_half(u).wait()
+                fetch_coef(u).wait()
+                buf = lax.rem(u, 2 * NB)
+                f = dot_stacked(cbuf[lax.rem(u, NB)].reshape(2 * LEVS, WAVES), lbuf[lax.div(buf, 2), lax.rem(buf, 2)], ((1,), (0,)))
+
+                @pl.when(u + 2 * NB < 2 * OWN)
+                def _():
+                    fetch_half(u + 2 * NB).start()
+
+                @pl.when(u + NB < 2 * OWN)
+                def _():
+                    fetch_coef(u + NB).start()
+
+                for j in range(SIDE):
+                    cols = f[:, j * LAT:(j + 1) * LAT]
+                    for r in range(2):
+                        packed = jnp.concatenate([cols[r * LEVS + q * KK:r * LEVS + (q + 1) * KK] for q in range(QQ)], axis=1)
+                        for kk in range(KK):
+                            both[kk, r, pl.ds((side * SIDE + j) * OWN + t, 1), :] = packed[kk:kk + 1]
+
+            if part == 0:
+                @pl.when(c == 0)
+                def _():
+                    barrier_wait()
+
+            for o in range(SIDE):
+                o += SIDE * (1 - part)
+                move(o, both.at[pl.ds(0, FIRST), :, block(target(o), c * CHUNK, CHUNK), :], frecv.at[pl.ds(0, FIRST), :, block(me, c * CHUNK, CHUNK), :], fs1.at[o], fr1.at[o])
 
     for kk in range(FIRST, KK):
         for o in range(DEVS):
             move(o, both.at[kk, :, block(target(o)), :], frecv.at[kk, :, block(me), :], fs2.at[kk, o], fr2.at[kk, o])
     for t in range(NB):
-        fetch_leg(t).start()
+        for half in range(2):
+            fetch_leg(t, half).start()
 
     def dst_rows(o, row, size):
         return pl.ds(pl.multiple_of(target(o) * (OWN // 2) + row, CHUNK), size)
@@ -226,25 +256,29 @@
         def _(i):
             t = c * CHUNK + i
             h = gather_rows(hrecv.at[:, par], row + i)
-            fetch_leg(t).wait()
-
-            spec_out[t] = dot_stacked(h, lbuf[lax.rem(t, NB)], ((1,), (1,))).reshape(2, LEVS, WAVES)
-
-            @pl.when(t + NB < EARLY_WAVES)
+            for half in range(2):
+                fetch_leg(t, half).wait()
+            spec_out[t] = dot_stacked(h, whole(lbuf, lax.rem(t, NB)), ((1,), (1,))).reshape(2, LEVS, WAVES)
+
+            @pl.when(t + NB < OWN)
             def _():
-                fetch_leg(t + NB).start()
+                for half in range(2):
+                    fetch_leg(t + NB, half).start()
 
     arrived(CHUNKS - 1)
+    for t in range(EARLY_WAVES, EARLY_WAVES + NB):
+        for half in range(2):
+            fetch_leg(t, half).wait()
     last_out[...] = hrecv[:, 1, :, :, 3 * CHUNK:4 * CHUNK, :]
     for o in range(1, DEVS):
         wait_for(both.at[:, :, block(target(o)), :], ssem.at[o])
 
 
-def finish(h_in, leg, grid_in, spec_in, grid_out, spec_out, lbuf, obuf, lsem, osem, gsem, ssem):
+def finish(h_in, leg_in, leg, grid_in, spec_in, grid_out, spec_out, lbuf, obuf, lsem, osem, gsem, ssem):
     me = lax.axis_index('w')
 
     def fetch_leg(i):
-        return pltpu.make_async_copy(leg.at[me * OWN + own_wave(EARLY_WAVES + i)], lbuf.at[i], lsem.at[i])
+        return pltpu.make_async_copy(leg.at[me * OWN + own_wave(EARLY_WAVES + i)], lbuf.at[i - NB], lsem.at[i - NB])
 
     def grid_copy(i):
         return pltpu.make_async_copy(grid_in.at[pl.ds(i * QQ, QQ)], grid_out.at[pl.ds(i * QQ, QQ)], gsem.at[i])
@@ -255,7 +289,7 @@
     def store(i):
         return pltpu.make_async_copy(obuf.at[i], spec_out.at[own_wave(EARLY_WAVES + i)], osem.at[i])
 
-    for i in range(CHUNK):
+    for i in range(NB, CHUNK):
         fetch_leg(i).start()
     for i in range(CHUNK):
         grid_copy(i).start()
@@ -264,11 +298,17 @@
     def _(t):
         spec_copy(t).start()
 
-    @pl.loop(0, CHUNK)
+    @pl.loop(0, NB)
+    def _(i):
+        block = whole(leg_in, lax.rem(EARLY_WAVES + i, NB))
+        obuf[i] = dot_stacked(gather_rows(h_in, i), block, ((1,), (1,))).reshape(2, LEVS, WAVES)
+        store(i).start()
+
+    @pl.loop(NB, CHUNK)
     def _(i):
         h = gather_rows(h_in, i)
         fetch_leg(i).wait()
-        obuf[i] = dot_stacked(h, lbuf[i], ((1,), (1,))).reshape(2, LEVS, WAVES)
+        obuf[i] = dot_stacked(h, lbuf[i - NB], ((1,), (1,))).reshape(2, LEVS, WAVES)
         store(i).start()
 
     @pl.loop(0, CHUNK)
@@ -304,7 +344,7 @@
 ANY = pl.BlockSpec(memory_space=pl.ANY)
 VM = pl.BlockSpec(memory_space=pltpu.VMEM)
 DMA = pltpu.SemaphoreType.DMA
-LIMIT = 42 * 1024 * 1024
+LIMIT = 35 * 1024 * 1024
 LIMIT_END = 18 * 1024 * 1024
 
 
@@ -312,41 +352,41 @@
     dft, dft_t = dft_tables()
 
     def per_device(coef, legendre, gauss_weight):
-        _, grid_mid, spec_mid, last = pl.pallas_call(
+        _, spec_mid, last, leg_last, grid_mid = pl.pallas_call(
             transform,
             out_shape=(
                 jax.ShapeDtypeStruct((KK, 2, WAVES, LANES), F32),
-                pltpu.VMEM((LEVS, LAT, LONS), F32),
                 pltpu.VMEM((EARLY_WAVES, 2, LEVS, WAVES), F32),
                 pltpu.VMEM((DEVS, KK, 2, CHUNK, LANES), F32),
+                pltpu.VMEM((NB, 2, WAVES, LANES), F32),
+                pltpu.VMEM((LEVS, LAT, LONS), F32),
             ),
             in_specs=[ANY, ANY, VM, VM, VM],
-            out_specs=(ANY, VM, VM, VM),
+            out_specs=(ANY, VM, VM, VM, VM),
             scratch_shapes=[
                 pltpu.VMEM((NB, 2, LEVS, WAVES), F32),
-                pltpu.VMEM((NB, WAVES, LATS), F32),
                 pltpu.VMEM((2, WAVES, LANES), F32),
                 pltpu.VMEM((KK, 2, WAVES, LANES), F32),
                 pltpu.VMEM((DEVS, 2, KK, 2, OWN // 2, LANES), F32),
-                DMA((NB,)), DMA((NB,)), DMA,
+                DMA((NB,)), DMA((2 * NB,)), DMA((NB, 2)), DMA,
                 DMA((DEVS,)), DMA((DEVS,)), DMA((KK, DEVS)), DMA((KK, DEVS)), DMA((DEVS,)), DMA((DEVS,)), DMA((CHUNKS, DEVS)),
             ],
             compiler_params=pltpu.CompilerParams(collective_id=0, has_side_effects=True, vmem_limit_bytes=LIMIT),
             name='transform',
-        )(coef, legendre, dft, dft_t, gauss_weight[None, :])
+        )(coef, legendre, dft, dft_t, gauss_weight)
         grid, spec_out = pl.pallas_call(
             finish,
             out_shape=(jax.ShapeDtypeStruct((LEVS, LAT, LONS), F32), jax.ShapeDtypeStruct((OWN, 2, LEVS, WAVES), F32)),
-            in_specs=[VM, ANY, ANY, ANY],
+            in_specs=[VM, VM, ANY, ANY, ANY],
             out_specs=(ANY, ANY),
             scratch_shapes=[
-                pltpu.VMEM((CHUNK, WAVES, LATS), F32),
+                pltpu.VMEM((CHUNK - NB, WAVES, LATS), F32),
                 pltpu.VMEM((CHUNK, 2, LEVS, WAVES), F32),
-                DMA((CHUNK,)), DMA((CHUNK,)), DMA((CHUNK,)), DMA((EARLY_WAVES,)),
+                DMA((CHUNK - NB,)), DMA((CHUNK,)), DMA((CHUNK,)), DMA((EARLY_WAVES,)),
             ],
             compiler_params=pltpu.CompilerParams(vmem_limit_bytes=LIMIT_END),
             name='finish',
-        )(last, legendre, grid_mid, spec_mid)
+        )(last, leg_last, legendre, grid_mid, spec_mid)
         return grid, spec_out
 
     return jax.shard_map(per_device, mesh=mesh, in_specs=(P('w', None, 'lev', None), P(None, None, None), P(None)), out_specs=(P('lev', 'w', None), P('w', None, 'lev', None)), check_vma=False)

time: 301 us -> 294 us (0.977)
  Pallas kernels: 298 us -> 293 us
    pallas_call x1, Pallas kernels: 14.2 us -> 9.14 us  [per_device(): pl.pallas_call(finish, out_shape=(jax.ShapeDtypeStruct((LEVS, LAT, LONS),...]
where the time goes in v6:
time: 294 us
  Pallas kernels  293 us (100%)
    pallas_call x1, Pallas kernels, per_device(): pl.pallas_call(transform, out_shape=(jax.ShapeDtypeStruct((KK, 2, WAVES,...  284 us
    pallas_call x1, Pallas kernels, per_device(): pl.pallas_call(finish, out_shape=(jax.ShapeDtypeStruct((LEVS, LAT, LONS),...  9.14 us

profile of v6, /device:TPU:1, one launch (start us, length us, event | category | flops | bytes accessed | tf_op | source)
XLA Modules:
  0.0 294.0 jit_solution(6049108950829131743)
XLA Ops:
  0.6 284.2 %transform.1 = (f32[8,2,512,384]{3,2,1,0:T(8,128)}, f32[56,2,32,512]{3,2,1,0:T(8,128)S(1)}, f32[8,8,2,8,384]{4,3,2,1,0:T(8,128)S(1)}, f32[5,2,512,384]{3,2,1,0:T(8,128)S(1)}, f32[32,96,1024]{2,1,0:T(8,128)S(1)}) custom-call(f32[64,2,32,512]{3,2,1,0:T(8,128)} %coef.1, f32[512,512,768]{2,1,0:T(8,128)} %leg.3, bf16[2,2,512,512]{3,2,1,0:T(8,128)(2,1)} %constant.4.clone.dft, ...), custom_call_target="tpu_custom_call" | custom-call | tf_op jit(solution)/shard_map/transform/pallas_call | solution.py:355
  284.8 9.1 %finish.1 = (f32[32,96,1024]{2,1,0:T(8,128)}, f32[64,2,32,512]{3,2,1,0:T(8,128)}) custom-call(f32[8,8,2,8,384]{4,3,2,1,0:T(8,128)S(1)} %get-tuple-element.6.h_in, f32[5,2,512,384]{3,2,1,0:T(8,128)S(1)} %get-tuple-element.7.leg_in, f32[512,512,768]{2,1,0:T(8,128)} %leg.3, f32[32,96,1024]{2,1,0:T(8,128)S(1)} %get-tuple-element.8.grid_in, ...), custom_call_target="tpu_custom_call" | custom-call | tf_op jit(solution)/shard_map/finish/pallas_call | solution.py:377

commit v7 on v6

--- a/solution.py
+++ b/solution.py
@@ -76,7 +76,7 @@
     return jnp.concatenate([lbuf[slot, 0], lbuf[slot, 1]], axis=1)
 
 
-def transform(coef, leg, dft, dft_t, weight, frecv, spec_out, last_out, lbuf, grid_out, cbuf, fbuf, both, hrecv, csem, hsem, lsem, fsem, fs1, fr1, fs2, fr2, ssem, asem, bsem):
+def transform(coef, leg, table, weight_in, frecv, spec_out, last_out, lbuf, grid_out, dft, dft_t, weight, cbuf, fbuf, both, hrecv, csem, hsem, lsem, fsem, fs1, fr1, fs2, fr2, ssem, asem, bsem, tsem):
     me = lax.axis_index('w')
     barrier_signal(me)
 
@@ -117,12 +117,6 @@
         else:
             pltpu.make_async_remote_copy(src_ref=src_ref, dst_ref=dst_ref, send_sem=send_sem, recv_sem=recv_sem, device_id={'w': target(o)}, device_id_type=pl.DeviceIdType.MESH).start()
 
-    weights = weight[...].reshape(1, LATS)
-    own_weight = weights[:, 0:LAT]
-    for d in range(1, DEVS):
-        own_weight = jnp.where(me == d, weights[:, d * LAT:(d + 1) * LAT], own_weight)
-    own_weight = jnp.concatenate([own_weight] * QQ, axis=1)
-
     def wait_for(part, sem):
         pltpu.make_async_copy(part, part, sem).wait()
 
@@ -130,6 +124,9 @@
         fetch_half(u).start()
     for u in range(NB):
         fetch_coef(u).start()
+    constants = (pltpu.make_async_copy(table, dft, tsem.at[0]), pltpu.make_async_copy(weight_in, weight, tsem.at[1]))
+    for copy in constants:
+        copy.start()
 
     @pl.loop(0, CHUNKS)
     def _(c):
@@ -175,6 +172,19 @@
     for t in range(NB):
         for half in range(2):
             fetch_leg(t, half).start()
+
+    for copy in constants:
+        copy.wait()
+    weights = weight[...].reshape(1, LATS)
+    own_weight = weights[:, 0:LAT]
+    for d in range(1, DEVS):
+        own_weight = jnp.where(me == d, weights[:, d * LAT:(d + 1) * LAT], own_weight)
+    own_weight = jnp.concatenate([own_weight] * QQ, axis=1)
+    rows = lax.broadcasted_iota(jnp.int32, (WAVES, 1), 0)
+    for par in range(2):
+        unscale = jnp.where(rows == 0, 1.0 * LONS, 1.0 * HALF) if par == 0 else 1.0 * HALF
+        for half in range(2):
+            dft_t[par, half] = (dft[par, half].astype(F32).T * unscale).astype(BF)
 
     def dst_rows(o, row, size):
         return pl.ds(pl.multiple_of(target(o) * (OWN // 2) + row, CHUNK), size)
@@ -338,7 +348,7 @@
         hi = x.astype(jnp.bfloat16)
         return np.stack([hi, (x - hi.astype(np.float32)).astype(jnp.bfloat16)], axis=1)
 
-    return halves(back * scale), halves(np.swapaxes(back, 1, 2))
+    return halves(back * scale)
 
 
 ANY = pl.BlockSpec(memory_space=pl.ANY)
@@ -349,7 +359,7 @@
 
 
 def solution(mesh):
-    dft, dft_t = dft_tables()
+    table = dft_tables()
 
     def per_device(coef, legendre, gauss_weight):
         _, spec_mid, last, leg_last, grid_mid = pl.pallas_call(
@@ -361,19 +371,22 @@
                 pltpu.VMEM((NB, 2, WAVES, LANES), F32),
                 pltpu.VMEM((LEVS, LAT, LONS), F32),
             ),
-            in_specs=[ANY, ANY, VM, VM, VM],
+            in_specs=[ANY, ANY, ANY, ANY],
             out_specs=(ANY, VM, VM, VM, VM),
             scratch_shapes=[
+                pltpu.VMEM((2, 2, HALF, WAVES), BF),
+                pltpu.VMEM((2, 2, WAVES, HALF), BF),
+                pltpu.VMEM((LATS,), F32),
                 pltpu.VMEM((NB, 2, LEVS, WAVES), F32),
                 pltpu.VMEM((2, WAVES, LANES), F32),
                 pltpu.VMEM((KK, 2, WAVES, LANES), F32),
                 pltpu.VMEM((DEVS, 2, KK, 2, OWN // 2, LANES), F32),
                 DMA((NB,)), DMA((2 * NB,)), DMA((NB, 2)), DMA,
-                DMA((DEVS,)), DMA((DEVS,)), DMA((KK, DEVS)), DMA((KK, DEVS)), DMA((DEVS,)), DMA((DEVS,)), DMA((CHUNKS, DEVS)),
+                DMA((DEVS,)), DMA((DEVS,)), DMA((KK, DEVS)), DMA((KK, DEVS)), DMA((DEVS,)), DMA((DEVS,)), DMA((CHUNKS, DEVS)), DMA((2,)),
             ],
             compiler_params=pltpu.CompilerParams(collective_id=0, has_side_effects=True, vmem_limit_bytes=LIMIT),
             name='transform',
-        )(coef, legendre, dft, dft_t, gauss_weight)
+        )(coef, legendre, table, gauss_weight)
         grid, spec_out = pl.pallas_call(
             finish,
             out_shape=(jax.ShapeDtypeStruct((LEVS, LAT, LONS), F32), jax.ShapeDtypeStruct((OWN, 2, LEVS, WAVES), F32)),

time: 294 us -> 292 us (level)
  no operation moved by 1% of the time
where the time goes in v7:
time: 292 us
  Pallas kernels  291 us (100%)
    pallas_call x1, Pallas kernels, per_device(): pl.pallas_call(transform, out_shape=(jax.ShapeDtypeStruct((KK, 2, WAVES,...  282 us
    pallas_call x1, Pallas kernels, per_device(): pl.pallas_call(finish, out_shape=(jax.ShapeDtypeStruct((LEVS, LAT, LONS),...  9.14 us

profile of v7, /device:TPU:1, one launch (start us, length us, event | category | flops | bytes accessed | tf_op | source)
XLA Modules:
  0.0 292.0 jit_solution(7117795673831691089)
XLA Ops:
  0.6 282.2 %transform.1 = (f32[8,2,512,384]{3,2,1,0:T(8,128)}, f32[56,2,32,512]{3,2,1,0:T(8,128)S(1)}, f32[8,8,2,8,384]{4,3,2,1,0:T(8,128)S(1)}, f32[5,2,512,384]{3,2,1,0:T(8,128)S(1)}, f32[32,96,1024]{2,1,0:T(8,128)S(1)}) custom-call(f32[64,2,32,512]{3,2,1,0:T(8,128)} %coef.1, f32[512,512,768]{2,1,0:T(8,128)} %leg.3, bf16[2,2,512,512]{3,2,1,0:T(8,128)(2,1)} %constant.2.clone.table, ...), custom_call_target="tpu_custom_call" | custom-call | tf_op jit(solution)/shard_map/transform/pallas_call | solution.py:365
  282.8 9.1 %finish.1 = (f32[32,96,1024]{2,1,0:T(8,128)}, f32[64,2,32,512]{3,2,1,0:T(8,128)}) custom-call(f32[8,8,2,8,384]{4,3,2,1,0:T(8,128)S(1)} %get-tuple-element.6.h_in, f32[5,2,512,384]{3,2,1,0:T(8,128)S(1)} %get-tuple-element.7.leg_in, f32[512,512,768]{2,1,0:T(8,128)} %leg.3, f32[32,96,1024]{2,1,0:T(8,128)S(1)} %get-tuple-element.8.grid_in, ...), custom_call_target="tpu_custom_call" | custom-call | tf_op jit(solution)/shard_map/finish/pallas_call | solution.py:390

commit v8 on v7

--- a/solution.py
+++ b/solution.py
@@ -25,7 +25,7 @@
 CHUNKS = OWN // CHUNK
 FIRST = 6
 EARLY = 2
-AHEAD = 3
+AHEAD = 6
 EARLY_WAVES = OWN - CHUNK
 BF = jnp.bfloat16
 F32 = jnp.float32
@@ -120,10 +120,10 @@
     def wait_for(part, sem):
         pltpu.make_async_copy(part, part, sem).wait()
 
+    for u in range(NB):
+        fetch_coef(u).start()
     for u in range(2 * NB):
         fetch_half(u).start()
-    for u in range(NB):
-        fetch_coef(u).start()
     constants = (pltpu.make_async_copy(table, dft, tsem.at[0]), pltpu.make_async_copy(weight_in, weight, tsem.at[1]))
     for copy in constants:
         copy.start()

time: 292 us -> 292 us (level)
  no operation moved by 1% of the time
where the time goes in v8:
time: 292 us
  Pallas kernels  291 us (100%)
    pallas_call x1, Pallas kernels, per_device(): pl.pallas_call(transform, out_shape=(jax.ShapeDtypeStruct((KK, 2, WAVES,...  282 us
    pallas_call x1, Pallas kernels, per_device(): pl.pallas_call(finish, out_shape=(jax.ShapeDtypeStruct((LEVS, LAT, LONS),...  9.14 us

profile of v8, /device:TPU:1, one launch (start us, length us, event | category | flops | bytes accessed | tf_op | source)
XLA Modules:
  0.0 292.0 jit_solution(10888755780976283247)
XLA Ops:
  0.6 282.2 %transform.1 = (f32[8,2,512,384]{3,2,1,0:T(8,128)}, f32[56,2,32,512]{3,2,1,0:T(8,128)S(1)}, f32[8,8,2,8,384]{4,3,2,1,0:T(8,128)S(1)}, f32[5,2,512,384]{3,2,1,0:T(8,128)S(1)}, f32[32,96,1024]{2,1,0:T(8,128)S(1)}) custom-call(f32[64,2,32,512]{3,2,1,0:T(8,128)} %coef.1, f32[512,512,768]{2,1,0:T(8,128)} %leg.3, bf16[2,2,512,512]{3,2,1,0:T(8,128)(2,1)} %constant.2.clone.table, ...), custom_call_target="tpu_custom_call" | custom-call | tf_op jit(solution)/shard_map/transform/pallas_call | solution.py:365
  282.8 9.1 %finish.1 = (f32[32,96,1024]{2,1,0:T(8,128)}, f32[64,2,32,512]{3,2,1,0:T(8,128)}) custom-call(f32[8,8,2,8,384]{4,3,2,1,0:T(8,128)S(1)} %get-tuple-element.6.h_in, f32[5,2,512,384]{3,2,1,0:T(8,128)S(1)} %get-tuple-element.7.leg_in, f32[512,512,768]{2,1,0:T(8,128)} %leg.3, f32[32,96,1024]{2,1,0:T(8,128)S(1)} %get-tuple-element.8.grid_in, ...), custom_call_target="tpu_custom_call" | custom-call | tf_op jit(solution)/shard_map/finish/pallas_call | solution.py:390

commit v9 on v8

--- a/solution.py
+++ b/solution.py
@@ -18,6 +18,7 @@
 HALF = LONS // 2
 KK = 8
 QQ = 4
+ORDER = (6, 5, 7, 4, 2, 3, 1, 0)
 SIDE = 4
 LANES = QQ * LAT
 CHUNK = 8
@@ -162,12 +163,11 @@
                 def _():
                     barrier_wait()
 
-            for o in range(SIDE):
-                o += SIDE * (1 - part)
+            for o in ORDER[part * SIDE:(part + 1) * SIDE]:
                 move(o, both.at[pl.ds(0, FIRST), :, block(target(o), c * CHUNK, CHUNK), :], frecv.at[pl.ds(0, FIRST), :, block(me, c * CHUNK, CHUNK), :], fs1.at[o], fr1.at[o])
 
     for kk in range(FIRST, KK):
-        for o in range(DEVS):
+        for o in ORDER:
             move(o, both.at[kk, :, block(target(o)), :], frecv.at[kk, :, block(me), :], fs2.at[kk, o], fr2.at[kk, o])
     for t in range(NB):
         for half in range(2):
@@ -190,7 +190,7 @@
         return pl.ds(pl.multiple_of(target(o) * (OWN // 2) + row, CHUNK), size)
 
     def send_levels(kk):
-        for o in range(DEVS):
+        for o in ORDER:
             for par in range(2):
                 move(o, both.at[kk, :, dst_rows(o, par * (WAVES // 2), OWN // 2), :], hrecv.at[me, par, kk], ssem.at[o], asem.at[o])
 
@@ -200,7 +200,7 @@
 
     def send_chunk(c):
         row = lax.div(c, 4) * (WAVES // 2) + lax.rem(c, 4) * CHUNK
-        for o in range(DEVS):
+        for o in ORDER:
             move(o, both.at[pl.ds(EARLY, KK - EARLY), :, dst_rows(o, row, CHUNK), :], chunk_at(hrecv.at[me], c), ssem.at[o], bsem.at[c, o])
 
     def arrived(c):

time: 292 us -> 292 us (level)
  no operation moved by 1% of the time
where the time goes in v9:
time: 292 us; the launch traced here: 291 us
  Pallas kernels  290 us (99%)
    pallas_call x1, Pallas kernels, per_device(): pl.pallas_call(transform, out_shape=(jax.ShapeDtypeStruct((KK, 2, WAVES,...  281 us
    pallas_call x1, Pallas kernels, per_device(): pl.pallas_call(finish, out_shape=(jax.ShapeDtypeStruct((LEVS, LAT, LONS),...  9.14 us

profile of v9, /device:TPU:1, one launch (start us, length us, event | category | flops | bytes accessed | tf_op | source)
XLA Modules:
  0.0 290.8 jit_solution(5197979848411533267)
XLA Ops:
  0.6 281.0 %transform.1 = (f32[8,2,512,384]{3,2,1,0:T(8,128)}, f32[56,2,32,512]{3,2,1,0:T(8,128)S(1)}, f32[8,8,2,8,384]{4,3,2,1,0:T(8,128)S(1)}, f32[5,2,512,384]{3,2,1,0:T(8,128)S(1)}, f32[32,96,1024]{2,1,0:T(8,128)S(1)}) custom-call(f32[64,2,32,512]{3,2,1,0:T(8,128)} %coef.1, f32[512,512,768]{2,1,0:T(8,128)} %leg.3, bf16[2,2,512,512]{3,2,1,0:T(8,128)(2,1)} %constant.2.clone.table, ...), custom_call_target="tpu_custom_call" | custom-call | tf_op jit(solution)/shard_map/transform/pallas_call | solution.py:365
  281.7 9.1 %finish.1 = (f32[32,96,1024]{2,1,0:T(8,128)}, f32[64,2,32,512]{3,2,1,0:T(8,128)}) custom-call(f32[8,8,2,8,384]{4,3,2,1,0:T(8,128)S(1)} %get-tuple-element.6.h_in, f32[5,2,512,384]{3,2,1,0:T(8,128)S(1)} %get-tuple-element.7.leg_in, f32[512,512,768]{2,1,0:T(8,128)} %leg.3, f32[32,96,1024]{2,1,0:T(8,128)S(1)} %get-tuple-element.8.grid_in, ...), custom_call_target="tpu_custom_call" | custom-call | tf_op jit(solution)/shard_map/finish/pallas_call | solution.py:390

commit v10 on v9

--- a/solution.py
+++ b/solution.py
@@ -22,7 +22,7 @@
 SIDE = 4
 LANES = QQ * LAT
 CHUNK = 8
-NB = 5
+NB = 6
 CHUNKS = OWN // CHUNK
 FIRST = 6
 EARLY = 2
@@ -275,11 +275,13 @@
                 for half in range(2):
                     fetch_leg(t + NB, half).start()
 
-    arrived(CHUNKS - 1)
     for t in range(EARLY_WAVES, EARLY_WAVES + NB):
         for half in range(2):
             fetch_leg(t, half).wait()
-    last_out[...] = hrecv[:, 1, :, :, 3 * CHUNK:4 * CHUNK, :]
+    for o in (0, 6, 5, 7, 4, 2, 3, 1):
+        d = source(o)
+        wait_for(chunk_at(hrecv.at[d], CHUNKS - 1), bsem.at[CHUNKS - 1, o])
+        last_out[d] = hrecv[d, 1, :, :, 3 * CHUNK:4 * CHUNK, :]
     for o in range(1, DEVS):
         wait_for(both.at[:, :, block(target(o)), :], ssem.at[o])
 
@@ -354,7 +356,7 @@
 ANY = pl.BlockSpec(memory_space=pl.ANY)
 VM = pl.BlockSpec(memory_space=pltpu.VMEM)
 DMA = pltpu.SemaphoreType.DMA
-LIMIT = 35 * 1024 * 1024
+LIMIT = 35100 * 1024
 LIMIT_END = 18 * 1024 * 1024
 
 

time: 292 us -> 291 us (level)
  no operation moved by 1% of the time
where the time goes in v10:
time: 291 us; the launch traced here: 290 us
  Pallas kernels  290 us (100%)
    pallas_call x1, Pallas kernels, per_device(): pl.pallas_call(transform, out_shape=(jax.ShapeDtypeStruct((KK, 2, WAVES,...  281 us
    pallas_call x1, Pallas kernels, per_device(): pl.pallas_call(finish, out_shape=(jax.ShapeDtypeStruct((LEVS, LAT, LONS),...  8.55 us

profile of v10, /device:TPU:1, one launch (start us, length us, event | category | flops | bytes accessed | tf_op | source)
XLA Modules:
  0.0 290.3 jit_solution(2067711020211359832)
XLA Ops:
  0.6 281.1 %transform.1 = (f32[8,2,512,384]{3,2,1,0:T(8,128)}, f32[56,2,32,512]{3,2,1,0:T(8,128)S(1)}, f32[8,8,2,8,384]{4,3,2,1,0:T(8,128)S(1)}, f32[6,2,512,384]{3,2,1,0:T(8,128)S(1)}, f32[32,96,1024]{2,1,0:T(8,128)S(1)}) custom-call(f32[64,2,32,512]{3,2,1,0:T(8,128)} %coef.1, f32[512,512,768]{2,1,0:T(8,128)} %leg.3, bf16[2,2,512,512]{3,2,1,0:T(8,128)(2,1)} %constant.2.clone.table, ...), custom_call_target="tpu_custom_call" | custom-call | tf_op jit(solution)/shard_map/transform/pallas_call | solution.py:367
  281.8 8.6 %finish.1 = (f32[32,96,1024]{2,1,0:T(8,128)}, f32[64,2,32,512]{3,2,1,0:T(8,128)}) custom-call(f32[8,8,2,8,384]{4,3,2,1,0:T(8,128)S(1)} %get-tuple-element.6.h_in, f32[6,2,512,384]{3,2,1,0:T(8,128)S(1)} %get-tuple-element.7.leg_in, f32[512,512,768]{2,1,0:T(8,128)} %leg.3, f32[32,96,1024]{2,1,0:T(8,128)S(1)} %get-tuple-element.8.grid_in, ...), custom_call_target="tpu_custom_call" | custom-call | tf_op jit(solution)/shard_map/finish/pallas_call | solution.py:392
